TPU v7x, 16 devices: a 4x2x1 block of a 4x4x8 slice. The times are simulated.
16 devices in a mesh: dp: 2 (over y, z), tp: 8 (over x, core).
Axes of the slice: x: 4, y: 2, z: 1, core: 2. Of those that a mesh axis runs over, the one named last changes fastest.
The devices are a block of a 4x4x8 slice.
Arguments:
- hidden: bfloat16 [256, 5120], P('dp'), parts along dimension 0
- positions: int32 [256], P('dp'), parts along dimension 0
- k_cache: bfloat16 [2, 256, 64, 8, 128], P(None, 'dp', None, 'tp'), parts along dimension 1
- v_cache: bfloat16 [2, 256, 64, 8, 128], P(None, 'dp', None, 'tp'), parts along dimension 1
- attn_norm: bfloat16 [2, 5120], replicated
- w_query: bfloat16 [2, 5120, 4096], P(None, None, 'tp')
- w_key: bfloat16 [2, 5120, 1024], P(None, None, 'tp')
- w_value: bfloat16 [2, 5120, 1024], P(None, None, 'tp')
- w_out: bfloat16 [2, 4096, 5120], P(None, 'tp')
- mlp_norm: bfloat16 [2, 5120], replicated
- w_gate: bfloat16 [2, 5120, 14336], P(None, None, 'tp')
- w_up: bfloat16 [2, 5120, 14336], P(None, None, 'tp')
- w_down: bfloat16 [2, 14336, 5120], P(None, 'tp')
Outputs:
- output 1: bfloat16 [256, 5120], P('dp'), parts along dimension 0
- output 2: bfloat16 [2, 256, 64, 8, 128], P(None, 'dp', None, 'tp'), parts along dimension 1
- output 3: bfloat16 [2, 256, 64, 8, 128], P(None, 'dp', None, 'tp'), parts along dimension 1
There are 2 independent parts. A program takes and returns all parts, laid end to end along the dimension named above; an argument that names none is the same for every part.
All inputs are finite; a program needn't handle non-finite values.
Results may differ from a plain program's by a relative error of at most 0.02.
Values are sent between devices in bfloat16 or wider.
A program may use at most 768 MiB of HBM per device.

v0:
```python
import math
import jax
import jax.numpy as jnp
from jax import lax
from jax.sharding import PartitionSpec as P


def rms_norm(hidden, weight):
    hidden_f32 = hidden.astype(jnp.float32)
    mean_sq = jnp.mean(hidden_f32 * hidden_f32, axis=-1, keepdims=True)
    return (hidden_f32 * lax.rsqrt(mean_sq + 1e-5) * weight.astype(jnp.float32)).astype(jnp.bfloat16)


def rope_tables(positions, head_dim):
    half_dim = head_dim // 2
    inv_freq = jnp.power(500000.0, -jnp.arange(half_dim, dtype=jnp.float32) * (2.0 / head_dim))
    wavelen = (2.0 * math.pi) / inv_freq
    smooth = (8192.0 / wavelen - 1.0) / 3.0
    blended = (1.0 - smooth) * inv_freq / 8.0 + smooth * inv_freq
    scaled = jnp.where(wavelen < 2048.0, inv_freq, jnp.where(wavelen > 8192.0, inv_freq / 8.0, blended))
    angles = positions.astype(jnp.float32)[:, None] * scaled[None, :]
    return jnp.cos(angles), jnp.sin(angles)


def apply_rope(vectors, cos_tab, sin_tab):
    half_dim = vectors.shape[-1] // 2
    vec_f32 = vectors.astype(jnp.float32)
    first = vec_f32[..., :half_dim]
    second = vec_f32[..., half_dim:]
    cos_b = cos_tab[:, None, :]
    sin_b = sin_tab[:, None, :]
    return jnp.concatenate([first * cos_b - second * sin_b, second * cos_b + first * sin_b], axis=-1).astype(jnp.bfloat16)


def attend_split(query, k_old, v_old, key_new, value_new, before):
    score_scale = query.shape[-1] ** -0.5
    scores = jnp.einsum('bkgd,bskd->bkgs', query, k_old, preferred_element_type=jnp.float32) * score_scale
    scores = jnp.where(before, scores, -jnp.inf)
    score_new = jnp.einsum('clhe,cle->clh', query, key_new, preferred_element_type=jnp.float32) * score_scale
    row_peak = jnp.maximum(jnp.max(scores, axis=-1), score_new)
    weight_old = jnp.exp(scores - row_peak[..., None])
    weight_new = jnp.exp(score_new - row_peak)
    inv_total = 1.0 / (jnp.sum(weight_old, axis=-1) + weight_new)
    prob_old = (weight_old * inv_total[..., None]).astype(jnp.bfloat16)
    prob_new = (weight_new * inv_total).astype(jnp.bfloat16)
    attn_out = jnp.einsum('bkgs,bskd->bkgd', prob_old, v_old, preferred_element_type=jnp.float32)
    attn_out = attn_out + prob_new[..., None].astype(jnp.float32) * value_new[:, :, None, :].astype(jnp.float32)
    return attn_out.astype(jnp.bfloat16)


def attention_block(hidden, norm_weight, wq_layer, wk_layer, wv_layer, wo_layer, k_old, v_old, cos_tab, sin_tab, before):
    batch_size = hidden.shape[0]
    kv_heads = k_old.shape[2]
    head_dim = k_old.shape[3]
    q_heads = wq_layer.shape[1] // head_dim
    normed = rms_norm(hidden, norm_weight)
    query = jnp.dot(normed, wq_layer, preferred_element_type=jnp.float32).astype(jnp.bfloat16)
    key_new = jnp.dot(normed, wk_layer, preferred_element_type=jnp.float32).astype(jnp.bfloat16)
    value_new = jnp.dot(normed, wv_layer, preferred_element_type=jnp.float32).astype(jnp.bfloat16)
    query = apply_rope(query.reshape(batch_size, q_heads, head_dim), cos_tab, sin_tab)
    key_new = apply_rope(key_new.reshape(batch_size, kv_heads, head_dim), cos_tab, sin_tab)
    value_new = value_new.reshape(batch_size, kv_heads, head_dim)
    attended = attend_split(query.reshape(batch_size, kv_heads, q_heads // kv_heads, head_dim), k_old, v_old, key_new, value_new, before)
    mixed = jnp.dot(attended.reshape(batch_size, q_heads * head_dim), wo_layer, preferred_element_type=jnp.float32)
    return mixed.astype(jnp.bfloat16), key_new, value_new


def mlp_block(hidden, norm_weight, wg_layer, wu_layer, wd_layer):
    normed = rms_norm(hidden, norm_weight)
    gate_proj = jnp.dot(normed, wg_layer, preferred_element_type=jnp.float32).astype(jnp.bfloat16)
    up_proj = jnp.dot(normed, wu_layer, preferred_element_type=jnp.float32).astype(jnp.bfloat16)
    activated = (jax.nn.silu(gate_proj.astype(jnp.float32)) * up_proj.astype(jnp.float32)).astype(jnp.bfloat16)
    return jnp.dot(activated, wd_layer, preferred_element_type=jnp.float32).astype(jnp.bfloat16)


def write_rows(cache, rows, positions):
    at_pos = (jnp.arange(cache.shape[2])[None, :] == positions[:, None])[None, :, :, None, None]
    return jnp.where(at_pos, rows[:, :, None], cache)


def solution(mesh):
    row_spec = P('dp', None)
    pos_spec = P('dp')
    cache_spec = P(None, 'dp', None, 'tp', None)
    norm_spec = P(None, None)
    col_spec = P(None, None, 'tp')
    split_rows = P(None, 'tp', None)

    def local_step(hidden, positions, k_cache, v_cache, attn_norm, w_query, w_key, w_value, w_out, mlp_norm, w_gate, w_up, w_down):
        cos_tab, sin_tab = rope_tables(positions, k_cache.shape[4])
        before = (jnp.arange(k_cache.shape[2])[None, :] < positions[:, None])[:, None, None, :]
        k_rows = []
        v_rows = []
        for layer in range(k_cache.shape[0]):
            part_out, key_new, value_new = attention_block(hidden, attn_norm[layer], w_query[layer], w_key[layer], w_value[layer], w_out[layer], k_cache[layer], v_cache[layer], cos_tab, sin_tab, before)
            hidden = hidden + lax.psum(part_out, 'tp')
            part_out = mlp_block(hidden, mlp_norm[layer], w_gate[layer], w_up[layer], w_down[layer])
            hidden = hidden + lax.psum(part_out, 'tp')
            k_rows.append(key_new)
            v_rows.append(value_new)
        k_out = write_rows(k_cache, jnp.stack(k_rows), positions)
        v_out = write_rows(v_cache, jnp.stack(v_rows), positions)
        return hidden, k_out, v_out

    return jax.shard_map(local_step, mesh=mesh, in_specs=(row_spec, pos_spec, cache_spec, cache_spec, norm_spec, col_spec, col_spec, col_spec, split_rows, norm_spec, col_spec, col_spec, split_rows), out_specs=(row_spec, cache_spec, cache_spec), check_vma=False)
```

profile of v0, /device:TPU:113, one launch (start us, length us, event | category | flops | bytes accessed | tf_op | source)
XLA Modules:
  0.0 334.9 jit_solution(3442496909341737744)
XLA Ops:
  7.3 0.7 convert_element_type.198
  7.9 0.7 iota_compare_fusion
  8.7 1.8 fusion.34
  10.5 0.8 slice_convert_fusion.1
  11.3 0.3 multiply_cosine_fusion
  11.6 2.4 fusion.139
  14.1 0.2 fusion.165
  14.4 1.9 fusion.180
  16.3 3.4 %fusion.109 = f32[128,512]{1,0:T(8,128)S(1)} fusion(bf16[2,5120,512]{2,1,0:T(8,128)(2,1)} %param.18, bf16[128,5120]{1,0:T(8,128)(2,1)S(1)} %copy-done, f32[5120]{0:T(1024)S(1)} %bitcast.197, f32[128]{0:T(128)S(1)} %add_rsqrt_fusion.3), kind=kOutput, calls=%fused_computation.95 | convolution fusion | flops 673841152 | bytes 6836736 | tf_op jit(solution)/shard_map/dot_general | solution.py:57
  19.8 0.3 subtract_convert_fusion.1
  20.1 0.3 multiply_reduce_fusion.1
  20.5 2.9 fusion.181
  23.5 0.1 copy.34
  23.6 0.4 fusion.146
  24.1 0.1 copy.36
  24.3 2.3 fusion.105
  26.7 4.4 %convolution_convert_fusion.1 = bf16[128,5120]{1,0:T(8,128)(2,1)} fusion(bf16[2,512,5120]{2,1,0:T(8,128)(2,1)} %param.21, bf16[16,8,4,128]{3,2,1,0:T(4,128)(2,1)S(1)} %bitcast.200), kind=kOutput, calls=%fused_computation.21 | convolution fusion | flops 671744000 | bytes 6684672 | tf_op jit(solution)/shard_map/dot_general | solution.py:64
  31.1 0.2 all-reduce.7.cloned.1.call-start
  31.4 55.8 %all-reduce.5.cloned.1.call-done = bf16[128,5120]{1,0:T(8,128)(2,1)} async-done(((bf16[128,5120]{1,0:T(8,128)(2,1)}), bf16[128,5120]{1,0:T(8,128)(2,1)}) %all-reduce.5.cloned.1.call-update) | async-done | bytes 1310736 | tf_op jit(solution)/shard_map/psum | solution.py:96
  87.3 1.9 fusion.37
  89.1 7.8 %fusion.49 = f32[128,1792]{1,0:T(8,128)S(1)} fusion(bf16[2,5120,1792]{2,1,0:T(8,128)(2,1)} %param.23, bf16[128,5120]{1,0:T(8,128)(2,1)S(1)} %get-tuple-element.8, f32[5120]{0:T(1024)S(1)} %bitcast.198, f32[128]{0:T(128)S(1)} %add_rsqrt_fusion.2), kind=kOutput, calls=%fused_computation.55 | convolution fusion | flops 2351890432 | bytes 20599296 | tf_op jit(solution)/shard_map/dot_general | solution.py:70
  97.0 8.0 %fusion.61 = bf16[128,1792]{1,0:T(8,128)(2,1)S(1)} fusion(bf16[2,5120,1792]{2,1,0:T(8,128)(2,1)} %param.24, f32[128,1792]{1,0:T(8,128)S(1)} %fusion.49, bf16[128,5120]{1,0:T(8,128)(2,1)S(1)} %get-tuple-element.8, f32[5120]{0:T(1024)S(1)} %bitcast.199, f32[128]{0:T(128)S(1)} %add_rsqrt_fusion.2), kind=kOutput, calls=%fused_computation.59 | convolution fusion | flops 2353266688 | bytes 21058048 | tf_op jit(solution)/shard_map/dot_general | solution.py:71
  104.9 10.0 %fusion.18 = bf16[128,5120]{1,0:T(8,128)(2,1)} fusion(bf16[128,1792]{1,0:T(8,128)(2,1)S(1)} %fusion.61, bf16[2,1792,5120]{2,1,0:T(8,128)(2,1)} %param.25), kind=kOutput, calls=%fused_computation.18 | convolution fusion | flops 2349465600 | bytes 20119552 | tf_op jit(solution)/shard_map/dot_general | solution.py:73
  115.0 0.3 all-reduce.9.cloned.1.call-start
  115.3 54.2 %all-reduce.7.cloned.1.call-done = bf16[128,5120]{1,0:T(8,128)(2,1)} async-done(((bf16[128,5120]{1,0:T(8,128)(2,1)}), bf16[128,5120]{1,0:T(8,128)(2,1)}) %all-reduce.7.cloned.1.call-update) | async-done | bytes 1310736 | tf_op jit(solution)/shard_map/psum | solution.py:98
  169.5 2.0 fusion.40
  171.6 0.8 fusion.133
  172.4 0.9 copy-done.3
  173.3 0.6 fusion.182
  173.9 3.4 %fusion.115 = f32[128,512]{1,0:T(8,128)S(1)} fusion(bf16[2,5120,512]{2,1,0:T(8,128)(2,1)} %param.18, bf16[128,5120]{1,0:T(8,128)(2,1)S(1)} %get-tuple-element.6, f32[5120]{0:T(1024)S(1)} %bitcast.194, f32[128]{0:T(128)S(1)} %add_rsqrt_fusion.1), kind=kOutput, calls=%fused_computation.97 | convolution fusion | flops 673841152 | bytes 6836736 | tf_op jit(solution)/shard_map/dot_general | solution.py:57
  177.3 0.2 fusion.169
  177.7 0.3 subtract_convert_fusion
  178.0 2.9 fusion.183
  181.0 0.3 multiply_reduce_fusion
  181.4 0.1 copy.41
  181.6 0.4 fusion.147
  182.3 2.3 fusion.104
  184.6 4.4 %convolution_convert_fusion = bf16[128,5120]{1,0:T(8,128)(2,1)} fusion(bf16[2,512,5120]{2,1,0:T(8,128)(2,1)} %param.21, bf16[16,8,4,128]{3,2,1,0:T(4,128)(2,1)S(1)} %bitcast.201), kind=kOutput, calls=%fused_computation.20 | convolution fusion | flops 671744000 | bytes 6684672 | tf_op jit(solution)/shard_map/dot_general | solution.py:64
  189.1 0.3 all-reduce.11.cloned.1.call-start
  189.4 0.1 copy.46
  189.6 54.1 %all-reduce.9.cloned.1.call-done = bf16[128,5120]{1,0:T(8,128)(2,1)} async-done(((bf16[128,5120]{1,0:T(8,128)(2,1)}), bf16[128,5120]{1,0:T(8,128)(2,1)}) %all-reduce.9.cloned.1.call-update) | async-done | bytes 1310736 | tf_op jit(solution)/shard_map/psum | solution.py:96
  243.6 1.9 fusion.43
  245.5 7.8 %fusion.67 = f32[128,1792]{1,0:T(8,128)S(1)} fusion(bf16[2,5120,1792]{2,1,0:T(8,128)(2,1)} %param.23, bf16[128,5120]{1,0:T(8,128)(2,1)S(1)} %get-tuple-element.4, f32[5120]{0:T(1024)S(1)} %bitcast.190, f32[128]{0:T(128)S(1)} %add_rsqrt_fusion), kind=kOutput, calls=%fused_computation.61 | convolution fusion | flops 2351890432 | bytes 20599296 | tf_op jit(solution)/shard_map/dot_general | solution.py:70
  253.3 7.9 %fusion.79 = bf16[128,1792]{1,0:T(8,128)(2,1)S(1)} fusion(bf16[2,5120,1792]{2,1,0:T(8,128)(2,1)} %param.24, f32[128,1792]{1,0:T(8,128)S(1)} %fusion.67, bf16[128,5120]{1,0:T(8,128)(2,1)S(1)} %get-tuple-element.4, f32[5120]{0:T(1024)S(1)} %bitcast.191, f32[128]{0:T(128)S(1)} %add_rsqrt_fusion), kind=kOutput, calls=%fused_computation.65 | convolution fusion | flops 2353266688 | bytes 21058048 | tf_op jit(solution)/shard_map/dot_general | solution.py:71
  261.3 9.8 %fusion.21 = bf16[128,5120]{1,0:T(8,128)(2,1)} fusion(bf16[128,1792]{1,0:T(8,128)(2,1)S(1)} %fusion.79, bf16[2,1792,5120]{2,1,0:T(8,128)(2,1)} %param.25), kind=kOutput, calls=%fused_computation.19 | convolution fusion | flops 2349465600 | bytes 20119552 | tf_op jit(solution)/shard_map/dot_general | solution.py:73
  271.2 7.4 %broadcast_select_fusion = (bf16[2,128,64,1,128]{4,2,3,1,0:T(8,128)(2,1)}, bf16[2,128,64,1,128]{4,2,3,1,0:T(8,128)(2,1)}) fusion(bf16[2,128,64,1,128]{4,2,3,1,0:T(8,128)(2,1)} %param.16, pred[128,64]{1,0:T(8,128)(4,1)S(1)} %get-tuple-element.29, bf16[2,128,128]{2,1,0:T(8,128)(2,1)S(1)} %maximum_bitcast_fusion.1, bf16[2,128,64,1,128]{4,2,3,1,0:T(8,128)(2,1)} %param.15, ...), kind=kLoop, calls=%fused_computation.32 | loop fusion | flops 4194304 | bytes 16916480 | tf_op jit(solution)/shard_map/jit(_where)/select_n | solution.py:78
  278.6 47.1 %all-reduce.11.cloned.1.call-done = bf16[128,5120]{1,0:T(8,128)(2,1)} async-done(((bf16[128,5120]{1,0:T(8,128)(2,1)}), bf16[128,5120]{1,0:T(8,128)(2,1)}) %all-reduce.11.cloned.1.call-update) | async-done | bytes 1310736 | tf_op jit(solution)/shard_map/psum | solution.py:98
  325.7 2.7 add.119
  (39 shorter events, 1.6 us)
Async XLA Ops:
  7.2 80.1 %all-reduce.5.cloned.1.call-start = ((), (), s32[]{:S(2)}) async-start(), calls=%async_computation | async-start | bytes 2621440 | tf_op jit(solution)/shard_map/psum | solution.py:96
  8.7 5.7 %copy-start = (bf16[128,5120]{1,0:T(8,128)(2,1)S(1)}, bf16[128,5120]{1,0:T(8,128)(2,1)}, u32[]{:S(2)}) copy-start(bf16[128,5120]{1,0:T(8,128)(2,1)} %param.13) | copy-start | bytes 3932164
  26.7 4.7 %copy-start.1 = (bf16[2,5120]{1,0:T(2,128)(2,1)S(1)}, bf16[2,5120]{1,0:T(2,128)(2,1)}, u32[]{:S(2)}) copy-start(bf16[2,5120]{1,0:T(2,128)(2,1)} %param.22) | copy-start | bytes 61444
  31.1 138.4 %all-reduce.7.cloned.1.call-start = ((), (), s32[]{:S(2)}) async-start(), calls=%async_computation.1 | async-start | bytes 2621440 | tf_op jit(solution)/shard_map/psum | solution.py:98
  115.0 128.7 %all-reduce.9.cloned.1.call-start = ((), (), s32[]{:S(2)}) async-start(), calls=%async_computation.2 | async-start | bytes 2621440 | tf_op jit(solution)/shard_map/psum | solution.py:96
  169.5 2.1 copy-start.2
  171.5 1.8 copy-start.3
  189.1 136.6 %all-reduce.11.cloned.1.call-start = ((), (), s32[]{:S(2)}) async-start(), calls=%async_computation.3 | async-start | bytes 2621440 | tf_op jit(solution)/shard_map/psum | solution.py:98
Sparse Core Ops, SparseCore 0:
  31.3 55.9 all-reduce.4
  115.1 54.3 all-reduce.6
  189.2 54.3 all-reduce.8
  271.3 54.3 all-reduce.10
where the time goes:
time: 338 us; the launch traced here: 335 us
  waiting for transfers between devices  211 us (62%)
  matrix products  83.1 us (25%)
  other arithmetic  22.7 us (7%)
  between operations  14.1 us (4%)
    psum x4, waiting for transfers between devices, local_step(): hidden = hidden + lax.psum(part_out, 'tp')  211 us
    dot_general x2, matrix products, mlp_block(): jnp.dot(activated, wd_layer, preferred_element_type=jnp.float32)  19.8 us
    dot_general x2, matrix products, mlp_block(): jnp.dot(normed, wu_layer, preferred_element_type=jnp.float32)  15.9 us
    dot_general x2, matrix products, mlp_block(): jnp.dot(normed, wg_layer, preferred_element_type=jnp.float32)  15.7 us
    dot_general x2, matrix products, attention_block(): jnp.dot(attended.reshape(batch_size, q_heads * head_dim), wo_layer, prefe...  8.81 us
    reduce_sum x4, other arithmetic, rms_norm(): mean_sq = jnp.mean(hidden_f32 * hidden_f32, axis=-1, keepdims=True)  7.49 us
    select_n x1, other arithmetic, write_rows(): return jnp.where(at_pos, rows[:, :, None], cache)  7.39 us
    dot_general x2, matrix products, attention_block(): jnp.dot(normed, wq_layer, preferred_element_type=jnp.float32)  6.76 us
  transfers between devices with their start and end apart: 4, of which 4 were waited for; matrix products, arithmetic and copies ran while one was open for 2% of the time, Pallas kernels for 0%

commit v1 on v0

--- a/solution.py
+++ b/solution.py
@@ -1,7 +1,10 @@
+import functools
 import math
 import jax
 import jax.numpy as jnp
 from jax import lax
+from jax.experimental import pallas as pl
+from jax.experimental.pallas import tpu as pltpu
 from jax.sharding import PartitionSpec as P
 
 
@@ -48,12 +51,11 @@
     return attn_out.astype(jnp.bfloat16)
 
 
-def attention_block(hidden, norm_weight, wq_layer, wk_layer, wv_layer, wo_layer, k_old, v_old, cos_tab, sin_tab, before):
-    batch_size = hidden.shape[0]
+def attention_block(normed, wq_layer, wk_layer, wv_layer, k_old, v_old, cos_tab, sin_tab, before):
+    batch_size = normed.shape[0]
     kv_heads = k_old.shape[2]
     head_dim = k_old.shape[3]
     q_heads = wq_layer.shape[1] // head_dim
-    normed = rms_norm(hidden, norm_weight)
     query = jnp.dot(normed, wq_layer, preferred_element_type=jnp.float32).astype(jnp.bfloat16)
     key_new = jnp.dot(normed, wk_layer, preferred_element_type=jnp.float32).astype(jnp.bfloat16)
     value_new = jnp.dot(normed, wv_layer, preferred_element_type=jnp.float32).astype(jnp.bfloat16)
@@ -61,16 +63,251 @@
     key_new = apply_rope(key_new.reshape(batch_size, kv_heads, head_dim), cos_tab, sin_tab)
     value_new = value_new.reshape(batch_size, kv_heads, head_dim)
     attended = attend_split(query.reshape(batch_size, kv_heads, q_heads // kv_heads, head_dim), k_old, v_old, key_new, value_new, before)
-    mixed = jnp.dot(attended.reshape(batch_size, q_heads * head_dim), wo_layer, preferred_element_type=jnp.float32)
-    return mixed.astype(jnp.bfloat16), key_new, value_new
-
-
-def mlp_block(hidden, norm_weight, wg_layer, wu_layer, wd_layer):
-    normed = rms_norm(hidden, norm_weight)
-    gate_proj = jnp.dot(normed, wg_layer, preferred_element_type=jnp.float32).astype(jnp.bfloat16)
-    up_proj = jnp.dot(normed, wu_layer, preferred_element_type=jnp.float32).astype(jnp.bfloat16)
-    activated = (jax.nn.silu(gate_proj.astype(jnp.float32)) * up_proj.astype(jnp.float32)).astype(jnp.bfloat16)
-    return jnp.dot(activated, wd_layer, preferred_element_type=jnp.float32).astype(jnp.bfloat16)
+    return attended.reshape(batch_size, q_heads * head_dim), key_new, value_new
+
+
+PIECES = 4
+TILE = 256
+
+
+def mlp_kernel(layer, last, chips, attn_ref, res_ref, norm_mlp_ref, norm_next_ref, wo_hbm, wg_hbm, wu_hbm, wd_hbm, *rest):
+    if last:
+        out_ref, rest = rest[0], rest[1:]
+    else:
+        out_ref, own_ref, rest = rest[0], rest[1], rest[2:]
+    (o_buf, g_buf, u_buf, d_buf, full, part, act, res, own_h, swap_in, summed, relay_in, relay_out, comb_in, direct_in,
+     w_sem, io_sem, rs_send, rs_recv, ag_send, ag_recv) = rest
+    rows, width = full.shape
+    piece = width // PIECES
+    half_rows = rows // 2
+    own_rows = half_rows // chips
+    half = width // 2
+    me = lax.axis_index('tp')
+    core = lax.rem(me, 2)
+    chip = me // 2
+    partner = me + 1 - 2 * core
+    right = 2 * lax.rem(chip + 1, chips) + core
+    left = 2 * lax.rem(chip + chips - 1, chips) + core
+    row0 = pl.multiple_of(core * half_rows + chip * own_rows, own_rows)
+    n_gate = g_buf.shape[0]
+
+    def load_out(p):
+        return pltpu.make_async_copy(wo_hbm.at[layer, :, pl.ds(p * piece, piece)], o_buf.at[p], w_sem.at[p])
+
+    def load_down(p):
+        return pltpu.make_async_copy(wd_hbm.at[layer, :, pl.ds(p * piece, piece)], d_buf.at[p], w_sem.at[PIECES + p])
+
+    def load_gate(j):
+        cols = pl.ds(pl.multiple_of(j * TILE, TILE), TILE)
+        return pltpu.make_async_copy(wg_hbm.at[layer, :, cols], g_buf.at[j], w_sem.at[2 * PIECES + j])
+
+    def load_up(j):
+        cols = pl.ds(pl.multiple_of(j * TILE, TILE), TILE)
+        return pltpu.make_async_copy(wu_hbm.at[layer, :, cols], u_buf.at[j], w_sem.at[2 * PIECES + n_gate + j])
+
+    load_res = pltpu.make_async_copy(res_ref if last else res_ref.at[pl.ds(row0, own_rows)], res, io_sem.at[0])
+
+    for p in range(PIECES):
+        load_out(p).start()
+    load_res.start()
+    for j in range(n_gate):
+        load_gate(j).start()
+        load_up(j).start()
+    for p in range(PIECES):
+        load_down(p).start()
+
+    barrier = pltpu.get_barrier_semaphore()
+    for peer in (partner, right, left):
+        pl.semaphore_signal(barrier, inc=1, device_id={'tp': peer}, device_id_type=pl.DeviceIdType.MESH)
+    pl.semaphore_wait(barrier, 3)
+
+    def remote(src, dst, send_sem, recv_sem, peer):
+        return pltpu.make_async_remote_copy(src_ref=src, dst_ref=dst, send_sem=send_sem, recv_sem=recv_sem, device_id={'tp': peer}, device_id_type=pl.DeviceIdType.MESH)
+
+    other_rows = pl.ds(pl.multiple_of((1 - core) * half_rows, half_rows), half_rows)
+    my_rows = pl.ds(pl.multiple_of(core * half_rows, half_rows), half_rows)
+
+    def block(offset):
+        return pl.ds(pl.multiple_of(lax.rem(chip + offset, chips) * own_rows, own_rows), own_rows)
+
+    def reduce_scatter(lhs_ref, w_buf, load):
+        def swap(p):
+            return remote(part.at[p, other_rows], swap_in.at[p], rs_send.at[0, p], rs_recv.at[0, p], partner)
+
+        def relay(p):
+            return remote(summed.at[p, block(2)], relay_in.at[p], rs_send.at[1, p], rs_recv.at[1, p], right if p % 2 == 0 else left)
+
+        def direct(p):
+            return remote(summed.at[p, block(chips - 1 if p % 2 == 0 else 1)], direct_in.at[p], rs_send.at[2, p], rs_recv.at[2, p], left if p % 2 == 0 else right)
+
+        def combined(p):
+            return remote(relay_out.at[p], comb_in.at[p], rs_send.at[3, p], rs_recv.at[3, p], right if p % 2 == 0 else left)
+
+        def product(p):
+            load(p).wait()
+            for i in range(piece // TILE):
+                cols = pl.ds(i * TILE, TILE)
+                part[p, :, cols] = jnp.dot(lhs_ref[...], w_buf[p, :, cols], preferred_element_type=jnp.float32).astype(jnp.bfloat16)
+            swap(p).start()
+
+        def chip_sum(p):
+            swap(p).wait_recv()
+            summed[p] = (part[p, my_rows].astype(jnp.float32) + swap_in[p].astype(jnp.float32)).astype(jnp.bfloat16)
+            relay(p).start()
+            direct(p).start()
+
+        def pass_on(p):
+            relay(p).wait_recv()
+            mine = summed[p, block(1 if p % 2 == 0 else chips - 1)]
+            relay_out[p] = (mine.astype(jnp.float32) + relay_in[p].astype(jnp.float32)).astype(jnp.bfloat16)
+            combined(p).start()
+
+        product(0)
+        product(1)
+        chip_sum(0)
+        product(2)
+        chip_sum(1)
+        product(3)
+        pass_on(0)
+        chip_sum(2)
+        pass_on(1)
+        chip_sum(3)
+        pass_on(2)
+        pass_on(3)
+        sum_sq = jnp.zeros((own_rows, 1), jnp.float32)
+        for p in range(PIECES):
+            cols = pl.ds(p * piece, piece)
+            direct(p).wait_recv()
+            combined(p).wait_recv()
+            total = summed[p, block(0)].astype(jnp.float32) + direct_in[p].astype(jnp.float32) + comb_in[p].astype(jnp.float32)
+            new = res[:, cols].astype(jnp.float32) + total.astype(jnp.bfloat16).astype(jnp.float32)
+            new = new.astype(jnp.bfloat16)
+            res[:, cols] = new
+            new = new.astype(jnp.float32)
+            sum_sq = sum_sq + jnp.sum(new * new, axis=-1, keepdims=True)
+        for p in range(PIECES):
+            for copy in (swap(p), relay(p), direct(p), combined(p)):
+                copy.wait_send()
+        return sum_sq
+
+    def normalize(sum_sq, norm_ref):
+        scale = lax.rsqrt(sum_sq / width + 1e-5)
+        for p in range(PIECES):
+            cols = pl.ds(p * piece, piece)
+            own_h[:, cols] = (res[:, cols].astype(jnp.float32) * scale * norm_ref[:, cols].astype(jnp.float32)).astype(jnp.bfloat16)
+
+    def all_gather(src):
+        first, second = pl.ds(0, half), pl.ds(half, half)
+
+        def rows_of(offset, plane):
+            return pl.ds(pl.multiple_of(plane * half_rows + lax.rem(chip + offset, chips) * own_rows, own_rows), own_rows)
+
+        mine = rows_of(0, core)
+        to_right = [(src.at[:, first], full.at[mine, first]), (src.at[:, second], full.at[mine, second])]
+        to_left = [(src.at[:, second], full.at[mine, second]), (src.at[:, first], full.at[mine, first])]
+        from_left, from_right, across = rows_of(chips - 1, core), rows_of(1, core), rows_of(2, core)
+        arrived = [full.at[from_left, first], full.at[from_left, second], full.at[across, first],
+                   full.at[from_right, second], full.at[from_right, first], full.at[across, second]]
+        sends = [remote(*to_right[0], ag_send.at[0], ag_recv.at[0], right),
+                 remote(*to_right[1], ag_send.at[1], ag_recv.at[1], right),
+                 remote(arrived[0], arrived[0], ag_send.at[2], ag_recv.at[2], right),
+                 remote(*to_left[0], ag_send.at[3], ag_recv.at[3], left),
+                 remote(*to_left[1], ag_send.at[4], ag_recv.at[4], left),
+                 remote(arrived[3], arrived[3], ag_send.at[5], ag_recv.at[5], left),
+                 remote(src, full.at[mine], ag_send.at[6], ag_recv.at[6], partner)]
+        forward = [remote(arrived[i], arrived[i], ag_send.at[7 + i], ag_recv.at[7 + i], partner) for i in range(6)]
+        for i in (0, 3, 6, 1, 4):
+            sends[i].start()
+        full[mine, :] = src[...]
+        sends[0].wait_recv()
+        sends[2].start()
+        forward[0].start()
+        sends[3].wait_recv()
+        sends[5].start()
+        forward[3].start()
+        for i in (1, 4, 2, 5):
+            sends[i].wait_recv()
+            forward[i].start()
+        sends[6].wait_recv()
+        for i in range(6):
+            forward[i].wait_recv()
+        for copy in sends + forward:
+            copy.wait_send()
+
+    load_res.wait()
+    sum_sq = reduce_scatter(attn_ref, o_buf, load_out)
+    normalize(sum_sq, norm_mlp_ref)
+    all_gather(own_h)
+
+    def gate_up(j, carry):
+        load_gate(j).wait()
+        load_up(j).wait()
+        gate = jnp.dot(full[...], g_buf[j], preferred_element_type=jnp.float32).astype(jnp.bfloat16).astype(jnp.float32)
+        up = jnp.dot(full[...], u_buf[j], preferred_element_type=jnp.float32).astype(jnp.bfloat16).astype(jnp.float32)
+        act[:, pl.ds(pl.multiple_of(j * TILE, TILE), TILE)] = (gate * jax.nn.sigmoid(gate) * up).astype(jnp.bfloat16)
+        return carry
+
+    lax.fori_loop(0, n_gate, gate_up, 0)
+    sum_sq = reduce_scatter(act, d_buf, load_down)
+    if last:
+        all_gather(res)
+    else:
+        normalize(sum_sq, norm_next_ref)
+        own_ref[...] = res[...]
+        all_gather(own_h)
+    store = pltpu.make_async_copy(full, out_ref, io_sem.at[0])
+    store.start()
+    store.wait()
+
+
+def mlp_call(layer, last, chips, attended, residual, norm_mlp, norm_next, w_out, w_gate, w_up, w_down):
+    rows, inner = attended.shape
+    width = w_gate.shape[1]
+    ff = w_gate.shape[2]
+    piece = width // PIECES
+    own_rows = rows // 2 // chips
+    bf16 = jnp.bfloat16
+    vmem = pl.BlockSpec(memory_space=pltpu.VMEM)
+    hbm = pl.BlockSpec(memory_space=pl.ANY)
+    out_shape = [jax.ShapeDtypeStruct((rows, width), bf16)]
+    out_specs = [hbm]
+    if not last:
+        out_shape.append(jax.ShapeDtypeStruct((own_rows, width), bf16))
+        out_specs.append(vmem)
+    scratch = [
+        pltpu.VMEM((PIECES, inner, piece), bf16),
+        pltpu.VMEM((ff // TILE, width, TILE), bf16),
+        pltpu.VMEM((ff // TILE, width, TILE), bf16),
+        pltpu.VMEM((PIECES, ff, piece), bf16),
+        pltpu.VMEM((rows, width), bf16),
+        pltpu.VMEM((PIECES, rows, piece), bf16),
+        pltpu.VMEM((rows, ff), bf16),
+        pltpu.VMEM((own_rows, width), bf16),
+        pltpu.VMEM((own_rows, width), bf16),
+        pltpu.VMEM((PIECES, rows // 2, piece), bf16),
+        pltpu.VMEM((PIECES, rows // 2, piece), bf16),
+        pltpu.VMEM((PIECES, own_rows, piece), bf16),
+        pltpu.VMEM((PIECES, own_rows, piece), bf16),
+        pltpu.VMEM((PIECES, own_rows, piece), bf16),
+        pltpu.VMEM((PIECES, own_rows, piece), bf16),
+        pltpu.SemaphoreType.DMA((2 * PIECES + 2 * (ff // TILE),)),
+        pltpu.SemaphoreType.DMA((1,)),
+        pltpu.SemaphoreType.DMA((4, PIECES)),
+        pltpu.SemaphoreType.DMA((4, PIECES)),
+        pltpu.SemaphoreType.DMA((13,)),
+        pltpu.SemaphoreType.DMA((13,)),
+    ]
+    weights = inner * width + 3 * width * ff
+    return pl.pallas_call(
+        functools.partial(mlp_kernel, layer, last, chips),
+        out_shape=out_shape,
+        in_specs=[vmem, hbm, vmem, vmem, hbm, hbm, hbm, hbm],
+        out_specs=out_specs,
+        scratch_shapes=scratch,
+        compiler_params=pltpu.CompilerParams(collective_id=layer, has_side_effects=True, vmem_limit_bytes=67043328),
+        cost_estimate=pl.CostEstimate(flops=2 * rows * weights, bytes_accessed=2 * weights, transcendentals=rows * ff),
+        name='mlp_layer',
+    )(attended, residual, norm_mlp, norm_next, w_out, w_gate, w_up, w_down)
 
 
 def write_rows(cache, rows, positions):
@@ -85,17 +322,24 @@
     norm_spec = P(None, None)
     col_spec = P(None, None, 'tp')
     split_rows = P(None, 'tp', None)
+    chips = mesh.shape['tp'] // 2
 
     def local_step(hidden, positions, k_cache, v_cache, attn_norm, w_query, w_key, w_value, w_out, mlp_norm, w_gate, w_up, w_down):
         cos_tab, sin_tab = rope_tables(positions, k_cache.shape[4])
         before = (jnp.arange(k_cache.shape[2])[None, :] < positions[:, None])[:, None, None, :]
         k_rows = []
         v_rows = []
-        for layer in range(k_cache.shape[0]):
-            part_out, key_new, value_new = attention_block(hidden, attn_norm[layer], w_query[layer], w_key[layer], w_value[layer], w_out[layer], k_cache[layer], v_cache[layer], cos_tab, sin_tab, before)
-            hidden = hidden + lax.psum(part_out, 'tp')
-            part_out = mlp_block(hidden, mlp_norm[layer], w_gate[layer], w_up[layer], w_down[layer])
-            hidden = hidden + lax.psum(part_out, 'tp')
+        layers = k_cache.shape[0]
+        normed, residual = rms_norm(hidden, attn_norm[0]), hidden
+        for layer in range(layers):
+            last = layer == layers - 1
+            attended, key_new, value_new = attention_block(normed, w_query[layer], w_key[layer], w_value[layer], k_cache[layer], v_cache[layer], cos_tab, sin_tab, before)
+            following = layer if last else layer + 1
+            outs = mlp_call(layer, last, chips, attended, residual, mlp_norm[layer:layer + 1], attn_norm[following:following + 1], w_out, w_gate, w_up, w_down)
+            if last:
+                hidden = outs[0]
+            else:
+                normed, residual = outs
             k_rows.append(key_new)
             v_rows.append(value_new)
         k_out = write_rows(k_cache, jnp.stack(k_rows), positions)

time: 338 us -> 197 us (0.58)
  waiting for transfers between devices: 211 us -> 0 us
  Pallas kernels: 0 us -> 147 us
  matrix products: 83.1 us -> 26.5 us
  between operations: 14.1 us -> 1.05 us
  other arithmetic: 22.7 us -> 16.3 us
    psum x4 -> x0, waiting for transfers between devices: 211 us -> none  [local_step(): hidden = hidden + lax.psum(part_out, 'tp')]
    pallas_call x0 -> x2, Pallas kernels: none -> 147 us  [mlp_call(): pl.pallas_call(functools.partial(mlp_kernel, layer, last, chips), out_sha...]
    dot_general x8 -> x0, matrix products: 60.2 us -> none  [the longest x2 19.8 us: mlp_block(): jnp.dot(activated, wd_layer, preferred_element_type=jnp.float32)]
    reduce_sum x4 -> x1, other arithmetic: 7.49 us -> 1.75 us  [rms_norm(): mean_sq = jnp.mean(hidden_f32 * hidden_f32, axis=-1, keepdims=True)]
  transfers between devices with their start and end apart: 4 -> 0, of which waited for: 4 -> 0; matrix products, arithmetic and copies ran while one was open for 2% -> 0% of each run, Pallas kernels for 0% -> 0%
where the time goes in v1:
time: 197 us; the launch traced here: 196 us
  Pallas kernels  147 us (75%)
  matrix products  26.5 us (13%)
  other arithmetic  16.3 us (8%)
  local copies, waits for them, and re-layouts  5.26 us (3%)
    pallas_call x2, Pallas kernels, mlp_call(): pl.pallas_call(functools.partial(mlp_kernel, layer, last, chips), out_sha...  147 us
    select_n x1, other arithmetic, write_rows(): return jnp.where(at_pos, rows[:, :, None], cache)  7.53 us
    dot_general x2, matrix products, attention_block(): jnp.dot(normed, wq_layer, preferred_element_type=jnp.float32)  6.8 us
    dot_general x2, matrix products, attend_split(): jnp.einsum('bkgd,bskd->bkgs', query, k_old, preferred_element_type=jnp.fl...  5.86 us
    dot_general x2, matrix products, attention_block(): jnp.dot(normed, wk_layer, preferred_element_type=jnp.float32)  4.88 us
    dot_general x2, matrix products, attend_split(): jnp.einsum('bkgs,bskd->bkgd', prob_old, v_old, preferred_element_type=jnp...  4.65 us
    dot_general x2, matrix products, attention_block(): jnp.dot(normed, wv_layer, preferred_element_type=jnp.float32)  4.33 us

profile of v1, /device:TPU:113, one launch (start us, length us, event | category | flops | bytes accessed | tf_op | source)
XLA Modules:
  0.0 196.3 jit_solution(15203453781346846600)
XLA Ops:
  0.6 0.7 convert_element_type.132
  1.3 1.8 fusion.6
  3.1 1.4 iota_compare_fusion
  4.5 1.5 fusion.96
  6.0 2.4 %fusion.66 = f32[128,1,128]{0,2,1:T(8,128)S(1)} fusion(bf16[2,5120,128]{2,1,0:T(8,128)(2,1)} %param.19, bf16[128,5120]{1,0:T(8,128)(2,1)} %res_ref.1, f32[5120]{0:T(1024)S(1)} %bitcast.140, f32[128]{0:T(128)S(1)} %add_rsqrt_fusion), kind=kOutput, calls=%fused_computation.52 | convolution fusion | flops 170426368 | bytes 2707968 | tf_op jit(solution)/shard_map/dot_general | solution.py:60
  8.4 0.2 fusion.84
  8.6 0.6 copy-done.7
  9.2 0.1 copy.57
  9.3 2.5 %fusion.98 = (f32[128,128]{1,0:T(8,128)S(1)}, bf16[128,128]{1,0:T(8,128)(2,1)}) fusion(bf16[2,5120,128]{2,1,0:T(8,128)(2,1)} %param.20, bf16[128,5120]{1,0:T(8,128)(2,1)S(1)} %copy-done, f32[5120]{0:T(1024)S(1)} %bitcast.141, f32[128]{0:T(128)S(1)} %add_rsqrt_fusion), kind=kOutput, calls=%fused_computation.115 | convolution fusion | flops 170426368 | bytes 2740736 | tf_op jit(solution)/shard_map/dot_general | solution.py:61
  11.9 0.3 multiply_cosine_fusion
  12.2 3.4 %fusion.36 = f32[128,512]{1,0:T(8,128)S(1)} fusion(bf16[2,5120,512]{2,1,0:T(8,128)(2,1)} %param.18, bf16[128,5120]{1,0:T(8,128)(2,1)S(1)} %copy-done, f32[5120]{0:T(1024)S(1)} %bitcast.142, f32[128]{0:T(128)S(1)} %add_rsqrt_fusion), kind=kOutput, calls=%fused_computation.42 | convolution fusion | flops 673841152 | bytes 6836736 | tf_op jit(solution)/shard_map/dot_general | solution.py:59
  15.6 0.1 reshape.428
  15.8 0.3 subtract_convert_fusion.1
  16.0 0.3 multiply_reduce_fusion.1
  16.4 0.1 copy.51
  16.4 2.9 %fusion.99 = (f32[128,4]{1,0:T(8,128)S(1)}, f32[128,4,64]{2,1,0:T(4,128)S(1)}) fusion(bf16[2,128,64,1,128]{4,2,1,3,0:T(8,128)(2,1)} %bitcast.124, bf16[128,4,64]{2,1,0:T(4,128)(2,1)S(1)} %get-tuple-element.10, bf16[128,4,64]{2,1,0:T(4,128)(2,1)S(1)} %get-tuple-element.9, pred[128,64]{1,0:T(8,128)(4,1)S(1)} %get-tuple-element.28), kind=kOutput, calls=%fused_computation.116 | convolution fusion | flops 8748544 | bytes 2369536 | tf_op jit(solution)/shard_map/bkgd,bskd->bkgs/dot_general | solution.py:40
  19.4 0.1 copy.33
  19.5 0.1 copy.34
  19.6 0.4 fusion.69
  20.0 0.1 copy.35
  20.1 0.1 copy.36
  20.2 0.1 copy.38
  20.3 2.3 %fusion.32 = bf16[128,4,128]{2,1,0:T(4,128)(2,1)S(1)} fusion(bf16[2,128,64,1,128]{4,2,1,3,0:T(8,128)(2,1)} %bitcast.122, f32[128,4,64]{2,1,0:T(4,128)S(1)} %get-tuple-element.32, f32[128,128]{1,0:T(8,128)S(1)} %get-tuple-element.29, f32[128,4]{1,0:T(8,128)S(1)} %copy.38, f32[128,4]{1,0:T(8,128)S(1)} %copy.36, f32[128,4]{1,0:T(8,128)S(1)} %copy.34), kind=kOutput, calls=%fused_computation.40 | convolution fusion | flops 8683520 | bytes 2430976 | tf_op jit(solution)/shard_map/bkgs,bskd->bkgd/dot_general | solution.py:49
  22.7 0.7 copy.64
  23.3 74.2 %mlp_layer.2 = (bf16[128,5120]{1,0:T(8,128)(2,1)}, bf16[16,5120]{1,0:T(8,128)(2,1)}) custom-call(bf16[128,512]{1,0:T(8,128)(2,1)} %bitcast.126, bf16[128,5120]{1,0:T(8,128)(2,1)} %res_ref.1, bf16[1,5120]{1,0:T(2,128)(2,1)} %get-tuple-element.16.norm_mlp_ref, bf16[1,5120]{1,0:T(2,128)(2,1)} %get-tuple-element.38.norm_next_ref, bf16[2,512,5120]{2,1,0:T(8,128)(2,1)} %wo_hbm.3, ...), custom_call_target="tpu_custom_call" | custom-call | flops 7717519360 | bytes 60293120 | tf_op jit(solution)/shard_map/mlp_layer/pallas_call | solution.py:301
  97.6 2.4 %fusion.60 = f32[128,1,128]{0,2,1:T(8,128)S(1)} fusion(bf16[128,5120]{1,0:T(8,128)(2,1)} %get-tuple-element.5, bf16[2,5120,128]{2,1,0:T(8,128)(2,1)} %param.19), kind=kOutput, calls=%fused_computation.50 | convolution fusion | flops 167804928 | bytes 2686976 | tf_op jit(solution)/shard_map/dot_general | solution.py:60
  100.1 0.2 fusion.88
  100.3 0.7 copy.46
  101.1 0.1 copy.58
  101.2 1.8 fusion.100
  103.0 3.4 %fusion.42 = f32[128,512]{1,0:T(8,128)S(1)} fusion(bf16[128,5120]{1,0:T(8,128)(2,1)S(1)} %copy-done.2, bf16[2,5120,512]{2,1,0:T(8,128)(2,1)} %param.18), kind=kOutput, calls=%fused_computation.44 | convolution fusion | flops 671219712 | bytes 6815744 | tf_op jit(solution)/shard_map/dot_general | solution.py:59
  106.4 0.1 reshape.430
  106.5 0.3 subtract_convert_fusion
  106.8 0.3 multiply_reduce_fusion
  107.2 0.1 copy.56
  107.2 0.7 maximum_bitcast_fusion.1
  107.9 2.9 %fusion.101 = (f32[128,4]{1,0:T(8,128)S(1)}, f32[128,4,64]{2,1,0:T(4,128)S(1)}) fusion(bf16[2,128,64,1,128]{4,2,1,3,0:T(8,128)(2,1)} %bitcast.125, bf16[128,4,64]{2,1,0:T(4,128)(2,1)S(1)} %get-tuple-element.8, bf16[128,4,64]{2,1,0:T(4,128)(2,1)S(1)} %get-tuple-element.7, pred[128,64]{1,0:T(8,128)(4,1)S(1)} %copy-done.13), kind=kOutput, calls=%fused_computation.118 | convolution fusion | flops 8748544 | bytes 2369536 | tf_op jit(solution)/shard_map/bkgd,bskd->bkgs/dot_general | solution.py:40
  110.8 0.1 copy.40
  110.9 0.1 copy.41
  111.0 0.4 fusion.70
  111.4 0.1 copy.42
  111.5 0.1 copy.43
  111.6 0.1 copy.45
  111.7 2.3 %fusion.31 = bf16[128,4,128]{2,1,0:T(4,128)(2,1)S(1)} fusion(bf16[2,128,64,1,128]{4,2,1,3,0:T(8,128)(2,1)} %bitcast.123, f32[128,4,64]{2,1,0:T(4,128)S(1)} %get-tuple-element.36, f32[128,128]{1,0:T(8,128)S(1)} %get-tuple-element.33, f32[128,4]{1,0:T(8,128)S(1)} %copy.45, f32[128,4]{1,0:T(8,128)S(1)} %copy.43, f32[128,4]{1,0:T(8,128)S(1)} %copy.41), kind=kOutput, calls=%fused_computation.39 | convolution fusion | flops 8683520 | bytes 2430976 | tf_op jit(solution)/shard_map/bkgs,bskd->bkgd/dot_general | solution.py:49
  114.1 0.7 copy.63
  114.7 73.0 %mlp_layer.3 = bf16[128,5120]{1,0:T(8,128)(2,1)} custom-call(bf16[128,512]{1,0:T(8,128)(2,1)} %bitcast.127, bf16[16,5120]{1,0:T(8,128)(2,1)} %get-tuple-element.6.res_ref, bf16[1,5120]{1,0:T(2,128)(2,1)} %get-tuple-element.15.norm_mlp_ref, bf16[1,5120]{1,0:T(2,128)(2,1)} %get-tuple-element.38.norm_next_ref, bf16[2,512,5120]{2,1,0:T(8,128)(2,1)} %wo_hbm.3, ...), custom_call_target="tpu_custom_call" | custom-call | flops 7717519360 | bytes 60293120 | tf_op jit(solution)/shard_map/mlp_layer/pallas_call | solution.py:301
  187.7 7.5 %broadcast_select_fusion = (bf16[2,128,64,1,128]{4,2,3,1,0:T(8,128)(2,1)}, bf16[2,128,64,1,128]{4,2,3,1,0:T(8,128)(2,1)}) fusion(bf16[2,128,64,1,128]{4,2,3,1,0:T(8,128)(2,1)} %param.16, pred[128,64]{1,0:T(8,128)(4,1)} %get-tuple-element.27, bf16[2,128,128]{2,1,0:T(8,128)(2,1)} %maximum_bitcast_fusion.1, bf16[2,128,64,1,128]{4,2,3,1,0:T(8,128)(2,1)} %param.15, ...), kind=kLoop, calls=%fused_computation.6 | loop fusion | flops 4194304 | bytes 16916480 | tf_op jit(solution)/shard_map/jit(_where)/select_n | solution.py:315
  195.3 1.1 copy.66
  (44 shorter events, 0.2 us)
Async XLA Ops:
  1.3 10.6 %copy-start.14 = (f32[128]{0:T(128)}, f32[128]{0:T(128)S(1)}, u32[]{:S(2)}) copy-start(f32[128]{0:T(128)S(1)} %convert_element_type.132) | copy-start | bytes 1540
  1.3 10.6 %copy-start.16 = (f32[64]{0:T(128)}, f32[64]{0:T(128)S(1)}, u32[]{:S(2)}) copy-start(f32[64]{0:T(128)S(1)} %compare_select_fusion.1) | copy-start | bytes 772
  1.3 8.0 %copy-start = (bf16[128,5120]{1,0:T(8,128)(2,1)S(1)}, bf16[128,5120]{1,0:T(8,128)(2,1)}, u32[]{:S(2)}) copy-start(bf16[128,5120]{1,0:T(8,128)(2,1)} %res_ref.1) | copy-start | bytes 3932164
  4.5 12.0 %copy-start.12 = (pred[128,64]{1,0:T(8,128)(4,1)}, pred[128,64]{1,0:T(8,128)(4,1)S(1)}, u32[]{:S(2)}) copy-start(pred[128,64]{1,0:T(8,128)(4,1)S(1)} %get-tuple-element.28) | copy-start | bytes 24580
  8.6 0.6 copy-start.7
  8.6 0.6 copy-start.9
  12.2 3.5 %copy-start.3 = (f32[128,64]{1,0:T(8,128)}, f32[128,64]{1,0:T(8,128)S(1)}, u32[]{:S(2)}) copy-start(f32[128,64]{1,0:T(8,128)S(1)} %get-tuple-element.25) | copy-start | bytes 98308
  12.2 3.5 %copy-start.5 = (f32[128,64]{1,0:T(8,128)}, f32[128,64]{1,0:T(8,128)S(1)}, u32[]{:S(2)}) copy-start(f32[128,64]{1,0:T(8,128)S(1)} %get-tuple-element.26) | copy-start | bytes 98308
  97.6 2.5 %copy-start.15 = (f32[128]{0:T(128)S(1)}, f32[128]{0:T(128)}, u32[]{:S(2)}) copy-start(f32[128]{0:T(128)} %copy-done.14) | copy-start | bytes 1540
  97.6 2.5 %copy-start.17 = (f32[64]{0:T(128)S(1)}, f32[64]{0:T(128)}, u32[]{:S(2)}) copy-start(f32[64]{0:T(128)} %copy-done.16) | copy-start | bytes 772
  97.6 2.7 %copy-start.8 = (bf16[128,1,64]{0,2,1:T(8,128)(2,1)S(1)}, bf16[128,1,64]{0,2,1:T(8,128)(2,1)}, u32[]{:S(2)}) copy-start(bf16[128,1,64]{0,2,1:T(8,128)(2,1)} %copy-done.7) | copy-start | bytes 49156
  97.6 2.7 %copy-start.10 = (bf16[128,1,64]{0,2,1:T(8,128)(2,1)S(1)}, bf16[128,1,64]{0,2,1:T(8,128)(2,1)}, u32[]{:S(2)}) copy-start(bf16[128,1,64]{0,2,1:T(8,128)(2,1)} %copy-done.9) | copy-start | bytes 49156
  97.6 3.6 %copy-start.2 = (bf16[128,5120]{1,0:T(8,128)(2,1)S(1)}, bf16[128,5120]{1,0:T(8,128)(2,1)}, u32[]{:S(2)}) copy-start(bf16[128,5120]{1,0:T(8,128)(2,1)} %get-tuple-element.5) | copy-start | bytes 3932164
  103.0 3.5 %copy-start.4 = (f32[128,64]{1,0:T(8,128)S(1)}, f32[128,64]{1,0:T(8,128)}, u32[]{:S(2)}) copy-start(f32[128,64]{1,0:T(8,128)} %copy-done.3) | copy-start | bytes 98308
  103.0 3.5 %copy-start.6 = (f32[128,64]{1,0:T(8,128)S(1)}, f32[128,64]{1,0:T(8,128)}, u32[]{:S(2)}) copy-start(f32[128,64]{1,0:T(8,128)} %copy-done.5) | copy-start | bytes 98308
  103.0 4.2 %copy-start.11 = (bf16[128,128]{1,0:T(8,128)(2,1)S(1)}, bf16[128,128]{1,0:T(8,128)(2,1)}, u32[]{:S(2)}) copy-start(bf16[128,128]{1,0:T(8,128)(2,1)} %get-tuple-element.30) | copy-start | bytes 98308
  103.0 4.9 %copy-start.13 = (pred[128,64]{1,0:T(8,128)(4,1)S(1)}, pred[128,64]{1,0:T(8,128)(4,1)}, u32[]{:S(2)}) copy-start(pred[128,64]{1,0:T(8,128)(4,1)} %copy-done.12) | copy-start | bytes 24580
  187.7 7.5 %copy-start.1 = (bf16[128,5120]{1,0:T(8,128)(2,1)S(1)}, bf16[128,5120]{1,0:T(8,128)(2,1)}, u32[]{:S(2)}) copy-start(bf16[128,5120]{1,0:T(8,128)(2,1)} %mlp_layer.3) | copy-start | bytes 3932164

commit v2 on v1

v2 whole, which is shorter than its diff:
```python
import functools
import math
import jax
import jax.numpy as jnp
from jax import lax
from jax.experimental import pallas as pl
from jax.experimental.pallas import tpu as pltpu
from jax.sharding import PartitionSpec as P


def rope_tables(positions, head_dim):
    half_dim = head_dim // 2
    inv_freq = jnp.power(500000.0, -jnp.arange(half_dim, dtype=jnp.float32) * (2.0 / head_dim))
    wavelen = (2.0 * math.pi) / inv_freq
    smooth = (8192.0 / wavelen - 1.0) / 3.0
    blended = (1.0 - smooth) * inv_freq / 8.0 + smooth * inv_freq
    scaled = jnp.where(wavelen < 2048.0, inv_freq, jnp.where(wavelen > 8192.0, inv_freq / 8.0, blended))
    angles = positions.astype(jnp.float32)[:, None] * scaled[None, :]
    return jnp.cos(angles), jnp.sin(angles)


def attention_kernel(layer, first, x_ref, norm_ref, pos_smem, pos_ref, cos_ref, sin_ref, wq_hbm, wk_hbm, wv_hbm, k_hbm, v_hbm, *rest):
    if not first:
        rest = rest[2:]
    (out_ref, k_out, v_out, wq_buf, wkv_buf, k_buf, v_buf, h_buf, q_buf, kv_buf, w_sem, in_sem, out_sem) = rest
    rows, width = x_ref.shape
    inner = wq_buf.shape[1]
    seq, dim = k_buf.shape[1], k_buf.shape[2]
    heads = inner // dim
    chunk = width // CHUNKS
    groups = rows // GROUP

    def load_weights(i):
        ks = pl.ds(i * chunk, chunk)
        return (pltpu.make_async_copy(wq_hbm.at[layer, ks], wq_buf.at[ks], w_sem.at[0, i]),
                pltpu.make_async_copy(wk_hbm.at[layer, ks], wkv_buf.at[ks, pl.ds(0, dim)], w_sem.at[1, i]),
                pltpu.make_async_copy(wv_hbm.at[layer, ks], wkv_buf.at[ks, pl.ds(dim, dim)], w_sem.at[2, i]))

    load_k = pltpu.make_async_copy(k_hbm.at[layer], k_buf, in_sem.at[0])
    load_v = pltpu.make_async_copy(v_hbm.at[layer], v_buf, in_sem.at[1])
    for i in range(CHUNKS):
        for copy in load_weights(i):
            copy.start()
    load_k.start()
    load_v.start()

    if first:
        sum_sq = jnp.zeros((rows, 1), jnp.float32)
        for i in range(CHUNKS):
            part = x_ref[:, pl.ds(i * chunk, chunk)].astype(jnp.float32)
            sum_sq = sum_sq + jnp.sum(part * part, axis=-1, keepdims=True)
        scale = lax.rsqrt(sum_sq / width + 1e-5)
        for i in range(CHUNKS):
            cols = pl.ds(i * chunk, chunk)
            h_buf[:, cols] = (x_ref[:, cols].astype(jnp.float32) * scale * norm_ref[:, cols].astype(jnp.float32)).astype(jnp.bfloat16)
        h_ref = h_buf
    else:
        h_ref = x_ref

    for i in range(CHUNKS):
        for copy in load_weights(i):
            copy.wait()
        ks = pl.ds(i * chunk, chunk)
        q_part = jnp.dot(h_ref[:, ks], wq_buf[ks, :], preferred_element_type=jnp.float32)
        kv_part = jnp.dot(h_ref[:, ks], wkv_buf[ks, :], preferred_element_type=jnp.float32)
        if i == 0:
            q_buf[...] = q_part
            kv_buf[...] = kv_part
        else:
            q_buf[...] += q_part
            kv_buf[...] += kv_part

    def rounded(value):
        return value.astype(jnp.bfloat16).astype(jnp.float32)

    def rope(vec):
        vec = rounded(vec)
        half = dim // 2
        swapped = jnp.concatenate([vec[:, half:], vec[:, :half]], axis=-1)
        return rounded(vec * cos_ref[...] + swapped * sin_ref[...])

    for j in range(heads):
        cols = pl.ds(j * dim, dim)
        q_buf[:, cols] = rope(q_buf[:, cols])
    kv_buf[:, pl.ds(0, dim)] = rope(kv_buf[:, pl.ds(0, dim)])
    kv_buf[:, pl.ds(dim, dim)] = rounded(kv_buf[:, pl.ds(dim, dim)])

    load_k.wait()
    load_v.wait()

    def store(g):
        part = pl.ds(pl.multiple_of(g * GROUP, GROUP), GROUP)
        return (pltpu.make_async_copy(k_buf.at[part], k_out.at[layer, part], out_sem.at[0, g]),
                pltpu.make_async_copy(v_buf.at[part], v_out.at[layer, part], out_sem.at[1, g]))

    def attend(g, carry):
        base = pl.multiple_of(g * GROUP, GROUP)
        fresh = kv_buf[pl.ds(base, GROUP), :]
        for i in range(GROUP):
            pos = pos_smem[base + i]
            top = pl.multiple_of((pos // ROWS) * ROWS, ROWS)
            here = lax.broadcasted_iota(jnp.int32, (ROWS, dim), 0) == pos - top
            for buf, off in ((k_buf, 0), (v_buf, dim)):
                old = buf[base + i, pl.ds(top, ROWS), :].astype(jnp.float32)
                new = jnp.broadcast_to(fresh[i:i + 1, off:off + dim], (ROWS, dim))
                buf[base + i, pl.ds(top, ROWS), :] = jnp.where(here, new, old).astype(jnp.bfloat16)
        block = pl.ds(base, GROUP)
        query = jnp.concatenate([q_buf[block, pl.ds(j * dim, dim)] for j in range(heads)], axis=0).astype(jnp.bfloat16)
        keys = k_buf[block].reshape(GROUP * seq, dim)
        values = v_buf[block].reshape(GROUP * seq, dim)
        scores = lax.dot_general(query, keys, (((1,), (1,)), ((), ())), preferred_element_type=jnp.float32) * (dim ** -0.5)
        shape = (heads * GROUP, GROUP * seq)
        start = lax.rem(lax.broadcasted_iota(jnp.int32, shape, 0), GROUP) * seq
        col = lax.broadcasted_iota(jnp.int32, shape, 1)
        upto = start + jnp.concatenate([pos_ref[block, :]] * heads, axis=0)
        scores = jnp.where((col >= start) & (col <= upto), scores, -jnp.inf)
        weight = jnp.exp(scores - jnp.max(scores, axis=-1, keepdims=True))
        prob = (weight * (1.0 / jnp.sum(weight, axis=-1, keepdims=True))).astype(jnp.bfloat16)
        mixed = jnp.dot(prob, values, preferred_element_type=jnp.float32)
        for j in range(heads):
            q_buf[block, pl.ds(j * dim, dim)] = mixed[j * GROUP:(j + 1) * GROUP]
        for copy in store(g):
            copy.start()
        return carry

    lax.fori_loop(0, groups, attend, 0)
    out_ref[...] = q_buf[...].astype(jnp.bfloat16)

    def drain(g, carry):
        for copy in store(g):
            copy.wait()
        return carry

    lax.fori_loop(0, groups, drain, 0)


CHUNKS = 4
GROUP = 8
ROWS = 16


def attention_call(layer, x, norm, positions, cos_tab, sin_tab, w_query, w_key, w_value, k_cache, v_cache, k_done, v_done):
    rows, width = x.shape
    inner = w_query.shape[2]
    seq, dim = k_cache.shape[2], k_cache.shape[3]
    bf16 = jnp.bfloat16
    first = k_done is None
    vmem = pl.BlockSpec(memory_space=pltpu.VMEM)
    hbm = pl.BlockSpec(memory_space=pltpu.HBM)
    smem = pl.BlockSpec(memory_space=pltpu.SMEM)
    args = [x, norm, positions, positions[:, None], cos_tab, sin_tab, w_query, w_key, w_value, k_cache, v_cache]
    specs = [vmem, vmem, smem, vmem, vmem, vmem, hbm, hbm, hbm, hbm, hbm]
    aliases = {}
    if not first:
        aliases = {len(args): 1, len(args) + 1: 2}
        args += [k_done, v_done]
        specs += [hbm, hbm]
    weights = width * (inner + 2 * dim)
    return pl.pallas_call(
        functools.partial(attention_kernel, layer, first),
        out_shape=[jax.ShapeDtypeStruct((rows, inner), bf16), jax.ShapeDtypeStruct(k_cache.shape, bf16), jax.ShapeDtypeStruct(v_cache.shape, bf16)],
        in_specs=specs,
        out_specs=[vmem, hbm, hbm],
        scratch_shapes=[
            pltpu.VMEM((width, inner), bf16),
            pltpu.VMEM((width, 2 * dim), bf16),
            pltpu.VMEM((rows, seq, dim), bf16),
            pltpu.VMEM((rows, seq, dim), bf16),
            pltpu.VMEM((rows, width), bf16),
            pltpu.VMEM((rows, inner), jnp.float32),
            pltpu.VMEM((rows, 2 * dim), jnp.float32),
            pltpu.SemaphoreType.DMA((3, CHUNKS)),
            pltpu.SemaphoreType.DMA((2,)),
            pltpu.SemaphoreType.DMA((2, rows // GROUP)),
        ],
        input_output_aliases=aliases,
        compiler_params=pltpu.CompilerParams(vmem_limit_bytes=67043328),
        cost_estimate=pl.CostEstimate(flops=2 * rows * weights, bytes_accessed=2 * weights, transcendentals=rows * seq),
        name='attention_layer',
    )(*args)


PIECES = 4
TILE = 256


def mlp_kernel(layer, last, chips, attn_ref, res_ref, norm_mlp_ref, norm_next_ref, wo_hbm, wg_hbm, wu_hbm, wd_hbm, *rest):
    if last:
        out_ref, rest = rest[0], rest[1:]
    else:
        out_ref, own_ref, rest = rest[0], rest[1], rest[2:]
    (o_buf, g_buf, u_buf, d_buf, full, part, act, res, own_h, swap_in, summed, owner_in,
     w_sem, io_sem, rs_send, rs_recv, ag_send, ag_recv) = rest
    rows, width = full.shape
    piece = width // PIECES
    half_rows = rows // 2
    own_rows = half_rows // chips
    half = width // 2
    me = lax.axis_index('tp')
    core = lax.rem(me, 2)
    chip = me // 2
    partner = me + 1 - 2 * core
    peers = [2 * lax.rem(chip + hop, chips) + core for hop in range(chips)]
    hops = tuple(sorted(range(1, chips), key=lambda hop: -min(hop, chips - hop)))
    row0 = pl.multiple_of(core * half_rows + chip * own_rows, own_rows)
    n_gate = g_buf.shape[0]

    def load_out(p):
        return pltpu.make_async_copy(wo_hbm.at[layer, :, pl.ds(p * piece, piece)], o_buf.at[p], w_sem.at[p])

    def load_down(p):
        return pltpu.make_async_copy(wd_hbm.at[layer, :, pl.ds(p * piece, piece)], d_buf.at[p], w_sem.at[PIECES + p])

    def load_gate(j):
        cols = pl.ds(pl.multiple_of(j * TILE, TILE), TILE)
        return pltpu.make_async_copy(wg_hbm.at[layer, :, cols], g_buf.at[j], w_sem.at[2 * PIECES + j])

    def load_up(j):
        cols = pl.ds(pl.multiple_of(j * TILE, TILE), TILE)
        return pltpu.make_async_copy(wu_hbm.at[layer, :, cols], u_buf.at[j], w_sem.at[2 * PIECES + n_gate + j])

    load_res = pltpu.make_async_copy(res_ref if last else res_ref.at[pl.ds(row0, own_rows)], res, io_sem.at[0])

    for p in range(PIECES):
        load_out(p).start()
    load_res.start()

    def start_gate_up():
        for j in range(n_gate):
            load_gate(j).start()
            load_up(j).start()

    barrier = pltpu.get_barrier_semaphore()
    for peer in [partner] + peers[1:]:
        pl.semaphore_signal(barrier, inc=1, device_id={'tp': peer}, device_id_type=pl.DeviceIdType.MESH)
    pl.semaphore_wait(barrier, chips)

    def remote(src, dst, send_sem, recv_sem, peer):
        return pltpu.make_async_remote_copy(src_ref=src, dst_ref=dst, send_sem=send_sem, recv_sem=recv_sem, device_id={'tp': peer}, device_id_type=pl.DeviceIdType.MESH)

    other_rows = pl.ds(pl.multiple_of((1 - core) * half_rows, half_rows), half_rows)
    my_rows = pl.ds(pl.multiple_of(core * half_rows, half_rows), half_rows)

    def block(offset):
        return pl.ds(pl.multiple_of(lax.rem(chip + offset, chips) * own_rows, own_rows), own_rows)

    def reduce_scatter(lhs_ref, w_buf, load, after_loads):
        def swap(p):
            return remote(part.at[p, other_rows], swap_in.at[p], rs_send.at[0, p], rs_recv.at[0, p], partner)

        def to_owner(p, hop):
            return remote(summed.at[p, block(hop)], owner_in.at[hop - 1, p], rs_send.at[hop, p], rs_recv.at[hop, p], peers[hop])

        def product(p):
            load(p).wait()
            for i in range(piece // TILE):
                cols = pl.ds(i * TILE, TILE)
                part[p, :, cols] = jnp.dot(lhs_ref[...], w_buf[p, :, cols], preferred_element_type=jnp.float32).astype(jnp.bfloat16)
            swap(p).start()

        def chip_sum(p):
            swap(p).wait_recv()
            summed[p] = (part[p, my_rows].astype(jnp.float32) + swap_in[p].astype(jnp.float32)).astype(jnp.bfloat16)
            for hop in hops:
                to_owner(p, hop).start()

        product(0)
        product(1)
        chip_sum(0)
        for p in range(2, PIECES):
            product(p)
            chip_sum(p - 1)
        after_loads()
        chip_sum(PIECES - 1)
        sum_sq = jnp.zeros((own_rows, 1), jnp.float32)
        for p in range(PIECES):
            cols = pl.ds(p * piece, piece)
            total = summed[p, block(0)].astype(jnp.float32)
            for hop in range(1, chips):
                to_owner(p, hop).wait_recv()
                total = total + owner_in[hop - 1, p].astype(jnp.float32)
            new = res[:, cols].astype(jnp.float32) + total.astype(jnp.bfloat16).astype(jnp.float32)
            new = new.astype(jnp.bfloat16)
            res[:, cols] = new
            new = new.astype(jnp.float32)
            sum_sq = sum_sq + jnp.sum(new * new, axis=-1, keepdims=True)
        for p in range(PIECES):
            swap(p).wait_send()
            for hop in range(1, chips):
                to_owner(p, hop).wait_send()
        return sum_sq

    def normalize(sum_sq, norm_ref):
        scale = lax.rsqrt(sum_sq / width + 1e-5)
        for p in range(PIECES):
            cols = pl.ds(p * piece, piece)
            own_h[:, cols] = (res[:, cols].astype(jnp.float32) * scale * norm_ref[:, cols].astype(jnp.float32)).astype(jnp.bfloat16)

    def all_gather(src):
        def rows_of(offset):
            return pl.ds(pl.multiple_of(core * half_rows + lax.rem(chip + offset, chips) * own_rows, own_rows), own_rows)

        mine = rows_of(0)
        sends = [remote(src, full.at[mine], ag_send.at[hop], ag_recv.at[hop], peers[hop] if hop else partner) for hop in range(chips)]
        forward = [None]
        for hop in range(1, chips):
            landed = full.at[rows_of(chips - hop)]
            forward.append(remote(landed, landed, ag_send.at[chips + hop - 1], ag_recv.at[chips + hop - 1], partner))
        for hop in hops + (0,):
            sends[hop].start()
        full[mine, :] = src[...]
        for hop in (1, chips - 1) + tuple(range(2, chips - 1)):
            sends[hop].wait_recv()
            forward[hop].start()
        sends[0].wait_recv()
        for hop in range(1, chips):
            forward[hop].wait_recv()
        for copy in sends + forward[1:]:
            copy.wait_send()

    load_res.wait()
    sum_sq = reduce_scatter(attn_ref, o_buf, load_out, start_gate_up)
    for p in range(PIECES):
        load_down(p).start()
    normalize(sum_sq, norm_mlp_ref)
    all_gather(own_h)

    def gate_up(j, carry):
        load_gate(j).wait()
        load_up(j).wait()
        gate = jnp.dot(full[...], g_buf[j], preferred_element_type=jnp.float32).astype(jnp.bfloat16).astype(jnp.float32)
        up = jnp.dot(full[...], u_buf[j], preferred_element_type=jnp.float32).astype(jnp.bfloat16).astype(jnp.float32)
        act[:, pl.ds(pl.multiple_of(j * TILE, TILE), TILE)] = (gate * jax.nn.sigmoid(gate) * up).astype(jnp.bfloat16)
        return carry

    lax.fori_loop(0, n_gate, gate_up, 0)
    sum_sq = reduce_scatter(act, d_buf, load_down, lambda: None)
    if last:
        all_gather(res)
    else:
        normalize(sum_sq, norm_next_ref)
        own_ref[...] = res[...]
        all_gather(own_h)
    store = pltpu.make_async_copy(full, out_ref, io_sem.at[0])
    store.start()
    store.wait()


def mlp_call(layer, last, chips, attended, residual, norm_mlp, norm_next, w_out, w_gate, w_up, w_down):
    rows, inner = attended.shape
    width = w_gate.shape[1]
    ff = w_gate.shape[2]
    piece = width // PIECES
    own_rows = rows // 2 // chips
    bf16 = jnp.bfloat16
    vmem = pl.BlockSpec(memory_space=pltpu.VMEM)
    hbm = pl.BlockSpec(memory_space=pltpu.HBM)
    out_shape = [jax.ShapeDtypeStruct((rows, width), bf16)]
    out_specs = [hbm]
    if not last:
        out_shape.append(jax.ShapeDtypeStruct((own_rows, width), bf16))
        out_specs.append(vmem)
    scratch = [
        pltpu.VMEM((PIECES, inner, piece), bf16),
        pltpu.VMEM((ff // TILE, width, TILE), bf16),
        pltpu.VMEM((ff // TILE, width, TILE), bf16),
        pltpu.VMEM((PIECES, ff, piece), bf16),
        pltpu.VMEM((rows, width), bf16),
        pltpu.VMEM((PIECES, rows, piece), bf16),
        pltpu.VMEM((rows, ff), bf16),
        pltpu.VMEM((own_rows, width), bf16),
        pltpu.VMEM((own_rows, width), bf16),
        pltpu.VMEM((PIECES, rows // 2, piece), bf16),
        pltpu.VMEM((PIECES, rows // 2, piece), bf16),
        pltpu.VMEM((chips - 1, PIECES, own_rows, piece), bf16),
        pltpu.SemaphoreType.DMA((2 * PIECES + 2 * (ff // TILE),)),
        pltpu.SemaphoreType.DMA((1,)),
        pltpu.SemaphoreType.DMA((chips, PIECES)),
        pltpu.SemaphoreType.DMA((chips, PIECES)),
        pltpu.SemaphoreType.DMA((2 * chips - 1,)),
        pltpu.SemaphoreType.DMA((2 * chips - 1,)),
    ]
    weights = inner * width + 3 * width * ff
    return pl.pallas_call(
        functools.partial(mlp_kernel, layer, last, chips),
        out_shape=out_shape,
        in_specs=[vmem, hbm, vmem, vmem, hbm, hbm, hbm, hbm],
        out_specs=out_specs,
        scratch_shapes=scratch,
        compiler_params=pltpu.CompilerParams(collective_id=layer, has_side_effects=True, vmem_limit_bytes=67043328),
        cost_estimate=pl.CostEstimate(flops=2 * rows * weights, bytes_accessed=2 * weights, transcendentals=rows * ff),
        name='mlp_layer',
    )(attended, residual, norm_mlp, norm_next, w_out, w_gate, w_up, w_down)


def solution(mesh):
    row_spec = P('dp', None)
    pos_spec = P('dp')
    cache_spec = P(None, 'dp', None, 'tp', None)
    norm_spec = P(None, None)
    col_spec = P(None, None, 'tp')
    split_rows = P(None, 'tp', None)
    chips = mesh.shape['tp'] // 2

    def local_step(hidden, positions, k_cache, v_cache, attn_norm, w_query, w_key, w_value, w_out, mlp_norm, w_gate, w_up, w_down):
        layers, batch, seq, kv_heads, dim = k_cache.shape
        cos_tab, sin_tab = rope_tables(positions, dim)
        cos_tab = jnp.concatenate([cos_tab, cos_tab], axis=-1)
        sin_tab = jnp.concatenate([-sin_tab, sin_tab], axis=-1)
        k_cache = k_cache.reshape(layers, batch, seq, dim)
        v_cache = v_cache.reshape(layers, batch, seq, dim)
        k_out = v_out = None
        stream = residual = hidden
        for layer in range(layers):
            last = layer == layers - 1
            attended, k_out, v_out = attention_call(layer, stream, attn_norm[layer:layer + 1], positions, cos_tab, sin_tab, w_query, w_key, w_value, k_cache, v_cache, k_out, v_out)
            following = layer if last else layer + 1
            outs = mlp_call(layer, last, chips, attended, residual, mlp_norm[layer:layer + 1], attn_norm[following:following + 1], w_out, w_gate, w_up, w_down)
            if last:
                hidden = outs[0]
            else:
                stream, residual = outs
        shape = (layers, batch, seq, kv_heads, dim)
        return hidden, k_out.reshape(shape), v_out.reshape(shape)

    return jax.shard_map(local_step, mesh=mesh, in_specs=(row_spec, pos_spec, cache_spec, cache_spec, norm_spec, col_spec, col_spec, col_spec, split_rows, norm_spec, col_spec, col_spec, split_rows), out_specs=(row_spec, cache_spec, cache_spec), check_vma=False)
```

time: 197 us -> 153 us (0.78)
  matrix products: 26.5 us -> 0 us
  other arithmetic: 16.3 us -> 1.74 us
  Pallas kernels: 147 us -> 145 us
    pallas_call x2, Pallas kernels: 147 us -> 114 us  [mlp_call(): pl.pallas_call(functools.partial(mlp_kernel, layer, last, chips), out_sha...]
    pallas_call x0 -> x2, Pallas kernels: none -> 30.9 us  [attention_call(): pl.pallas_call(functools.partial(attention_kernel, layer, first), out_sha...]
    dot_general x10 -> x0, matrix products: 26.5 us -> none  [the longest x2 6.8 us: attention_block(): jnp.dot(normed, wq_layer, preferred_element_type=jnp.float32)]
    select_n x1 -> x0, other arithmetic: 7.53 us -> none  [write_rows(): return jnp.where(at_pos, rows[:, :, None], cache)]
    reduce_sum x3 -> x0, other arithmetic: 2.53 us -> none  [the longest x1 1.75 us: rms_norm(): mean_sq = jnp.mean(hidden_f32 * hidden_f32, axis=-1, keepdims=True)]
where the time goes in v2:
time: 153 us; the launch traced here: 152 us
  Pallas kernels  145 us (95%)
  local copies, waits for them, and re-layouts  5.35 us (3%)
  other arithmetic  1.74 us (1%)
    pallas_call x2, Pallas kernels, mlp_call(): pl.pallas_call(functools.partial(mlp_kernel, layer, last, chips), out_sha...  114 us
    pallas_call x2, Pallas kernels, attention_call(): pl.pallas_call(functools.partial(attention_kernel, layer, first), out_sha...  30.9 us

profile of v2, /device:TPU:113, one launch (start us, length us, event | category | flops | bytes accessed | tf_op | source)
XLA Modules:
  0.0 152.4 jit_solution(5567695412934546800)
XLA Ops:
  0.6 0.7 convert_element_type.3
  1.3 1.4 copy.18.pos_ref
  2.7 1.5 fusion.1
  4.2 0.3 fusion
  4.5 0.8 pad_maximum_fusion
  5.3 15.5 %attention_layer.2 = (bf16[128,512]{1,0:T(8,128)(2,1)}, bf16[2,128,64,128]{3,2,1,0:T(8,128)(2,1)}, bf16[2,128,64,128]{3,2,1,0:T(8,128)(2,1)}) custom-call(bf16[128,5120]{1,0:T(8,128)(2,1)} %res_ref.1, bf16[1,5120]{1,0:T(2,128)(2,1)} %get-tuple-element.31.norm_ref, s32[128]{0:T(128)} %pos_smem.3, s32[128,1]{1,0:T(8,128)} %copy.18.pos_ref, ...), custom_call_target="tpu_custom_call" | custom-call | flops 1006632960 | bytes 7864320 | tf_op jit(solution)/shard_map/attention_layer/pallas_call | solution.py:159
  20.8 58.7 %mlp_layer.2 = (bf16[128,5120]{1,0:T(8,128)(2,1)}, bf16[16,5120]{1,0:T(8,128)(2,1)}) custom-call(bf16[128,512]{1,0:T(8,128)(2,1)} %get-tuple-element.11.attn_ref, bf16[128,5120]{1,0:T(8,128)(2,1)} %res_ref.1, bf16[1,5120]{1,0:T(2,128)(2,1)} %get-tuple-element.23.norm_mlp_ref, bf16[1,5120]{1,0:T(2,128)(2,1)} %get-tuple-element.32.norm_next_ref.norm_ref, ...), custom_call_target="tpu_custom_call" | custom-call | flops 7717519360 | bytes 60293120 | tf_op jit(solution)/shard_map/mlp_layer/pallas_call | solution.py:384
  79.5 15.5 %attention_layer.3 = (bf16[128,512]{1,0:T(8,128)(2,1)}, bf16[2,128,64,128]{3,2,1,0:T(8,128)(2,1)}, bf16[2,128,64,128]{3,2,1,0:T(8,128)(2,1)}) custom-call(bf16[128,5120]{1,0:T(8,128)(2,1)} %get-tuple-element.12.x_ref, bf16[1,5120]{1,0:T(2,128)(2,1)} %get-tuple-element.32.norm_next_ref.norm_ref, ...), custom_call_target="tpu_custom_call", output_to_operand_aliasing={{1}: (11, {}), {2}: (12, {})} | custom-call | flops 1006632960 | bytes 7864320 | tf_op jit(solution)/shard_map/attention_layer/pallas_call | solution.py:159
  94.9 55.0 %mlp_layer.3 = bf16[128,5120]{1,0:T(8,128)(2,1)} custom-call(bf16[128,512]{1,0:T(8,128)(2,1)} %get-tuple-element.15.attn_ref, bf16[16,5120]{1,0:T(8,128)(2,1)} %get-tuple-element.16.res_ref, bf16[1,5120]{1,0:T(2,128)(2,1)} %get-tuple-element.22.norm_mlp_ref, bf16[1,5120]{1,0:T(2,128)(2,1)} %get-tuple-element.32.norm_next_ref.norm_ref, ...), custom_call_target="tpu_custom_call" | custom-call | flops 7717519360 | bytes 60293120 | tf_op jit(solution)/shard_map/mlp_layer/pallas_call | solution.py:384
  149.9 2.5 %copy.25 = bf16[128,5120]{1,0:T(8,128)(2,1)} copy(bf16[128,5120]{1,0:T(8,128)(2,1)} %mlp_layer.3) | data formatting | bytes 2621440
  (1 shorter events, 0.0 us)

commit v3 on v2

v3 whole, which is shorter than its diff:
```python
import functools
import math
import jax
import jax.numpy as jnp
from jax import lax
from jax.experimental import pallas as pl
from jax.experimental.pallas import tpu as pltpu
from jax.sharding import PartitionSpec as P


def rope_freqs(head_dim):
    half_dim = head_dim // 2
    inv_freq = jnp.power(500000.0, -jnp.arange(half_dim, dtype=jnp.float32) * (2.0 / head_dim))
    wavelen = (2.0 * math.pi) / inv_freq
    smooth = (8192.0 / wavelen - 1.0) / 3.0
    blended = (1.0 - smooth) * inv_freq / 8.0 + smooth * inv_freq
    scaled = jnp.where(wavelen < 2048.0, inv_freq, jnp.where(wavelen > 8192.0, inv_freq / 8.0, blended))
    return jnp.concatenate([scaled, scaled])[None, :]


def attention_kernel(layer, first, x_ref, norm_ref, pos_smem, pos_ref, freq_ref, wq_hbm, wk_hbm, wv_hbm, k_hbm, v_hbm, *rest):
    if not first:
        rest = rest[2:]
    (out_ref, k_out, v_out, wq_buf, wkv_buf, k_buf, v_buf, h_buf, q_buf, kv_buf, mix_buf, w_sem, in_sem, out_sem) = rest
    rows, width = x_ref.shape
    inner = wq_buf.shape[1]
    seq, dim = k_buf.shape[1], k_buf.shape[2]
    heads = inner // dim
    chunk = width // CHUNKS
    groups = rows // GROUP

    def load_weights(i):
        ks = pl.ds(i * chunk, chunk)
        return (pltpu.make_async_copy(wq_hbm.at[layer, ks], wq_buf.at[ks], w_sem.at[0, i]),
                pltpu.make_async_copy(wk_hbm.at[layer, ks], wkv_buf.at[ks, pl.ds(0, dim)], w_sem.at[1, i]),
                pltpu.make_async_copy(wv_hbm.at[layer, ks], wkv_buf.at[ks, pl.ds(dim, dim)], w_sem.at[2, i]))

    load_k = pltpu.make_async_copy(k_hbm.at[layer], k_buf, in_sem.at[0])
    load_v = pltpu.make_async_copy(v_hbm.at[layer], v_buf, in_sem.at[1])
    for i in range(CHUNKS):
        for copy in load_weights(i):
            copy.start()
    load_k.start()
    load_v.start()

    sum_sq = jnp.zeros((rows, 1), jnp.float32)
    for i in range(CHUNKS):
        part = x_ref[:, pl.ds(i * chunk, chunk)].astype(jnp.float32)
        sum_sq = sum_sq + jnp.sum(part * part, axis=-1, keepdims=True)
    scale = lax.rsqrt(sum_sq / width + 1e-5)
    for i in range(CHUNKS):
        cols = pl.ds(i * chunk, chunk)
        h_buf[:, cols] = (x_ref[:, cols].astype(jnp.float32) * scale * norm_ref[layer:layer + 1, cols].astype(jnp.float32)).astype(jnp.bfloat16)

    square = (rows, rows)
    diagonal = lax.broadcasted_iota(jnp.int32, square, 0) == lax.broadcasted_iota(jnp.int32, square, 1)
    column = jnp.sum(jnp.where(diagonal, jnp.broadcast_to(pos_ref[...].astype(jnp.float32), square), 0.0), axis=-1, keepdims=True)
    angles = column * freq_ref[...]
    lane = lax.broadcasted_iota(jnp.int32, (rows, dim), 1)
    cos_tab = jnp.cos(angles)
    sin_tab = jnp.where(lane < dim // 2, -jnp.sin(angles), jnp.sin(angles))

    for i in range(CHUNKS):
        for copy in load_weights(i):
            copy.wait()
        ks = pl.ds(i * chunk, chunk)
        q_part = jnp.dot(h_buf[:, ks], wq_buf[ks, :], preferred_element_type=jnp.float32)
        kv_part = jnp.dot(h_buf[:, ks], wkv_buf[ks, :], preferred_element_type=jnp.float32)
        if i == 0:
            q_buf[...] = q_part
            kv_buf[...] = kv_part
        else:
            q_buf[...] += q_part
            kv_buf[...] += kv_part

    def rounded(value):
        return value.astype(jnp.bfloat16).astype(jnp.float32)

    def rope(vec):
        vec = rounded(vec)
        half = dim // 2
        swapped = jnp.concatenate([vec[:, half:], vec[:, :half]], axis=-1)
        return rounded(vec * cos_tab + swapped * sin_tab)

    for j in range(heads):
        cols = pl.ds(j * dim, dim)
        q_buf[:, cols] = rope(q_buf[:, cols])
    kv_buf[:, pl.ds(0, dim)] = rope(kv_buf[:, pl.ds(0, dim)])
    kv_buf[:, pl.ds(dim, dim)] = rounded(kv_buf[:, pl.ds(dim, dim)])

    load_k.wait()
    load_v.wait()

    def store(g):
        part = pl.ds(pl.multiple_of(g * GROUP, GROUP), GROUP)
        return (pltpu.make_async_copy(k_buf.at[part], k_out.at[layer, part], out_sem.at[0, g]),
                pltpu.make_async_copy(v_buf.at[part], v_out.at[layer, part], out_sem.at[1, g]))

    def update(g, carry):
        base = pl.multiple_of(g * GROUP, GROUP)
        fresh = kv_buf[pl.ds(base, GROUP), :]
        for i in range(GROUP):
            pos = pos_smem[base + i]
            top = pl.multiple_of((pos // ROWS) * ROWS, ROWS)
            here = lax.broadcasted_iota(jnp.int32, (ROWS, dim), 0) == pos - top
            for buf, off in ((k_buf, 0), (v_buf, dim)):
                old = buf[base + i, pl.ds(top, ROWS), :].astype(jnp.float32)
                new = jnp.broadcast_to(fresh[i:i + 1, off:off + dim], (ROWS, dim))
                buf[base + i, pl.ds(top, ROWS), :] = jnp.where(here, new, old).astype(jnp.bfloat16)

        @pl.when(g > 0)
        def _():
            for copy in store(g - 1):
                copy.start()
        return carry

    lax.fori_loop(0, groups, update, 0)
    for copy in store(groups - 1):
        copy.start()

    request = lax.rem(lax.broadcasted_iota(jnp.int32, (heads * GROUP, 1), 0), GROUP)
    first_col = request * seq
    col = lax.broadcasted_iota(jnp.int32, (heads * GROUP, GROUP * seq), 1)

    def attend(step, carry):
        done = []
        for k in range(TOGETHER):
            base = pl.multiple_of((step * TOGETHER + k) * GROUP, GROUP)
            block = pl.ds(base, GROUP)
            last_col = first_col
            for i in range(GROUP):
                last_col = jnp.where(request == i, i * seq + pos_smem[base + i], last_col)
            query = jnp.concatenate([q_buf[block, pl.ds(j * dim, dim)] for j in range(heads)], axis=0).astype(jnp.bfloat16)
            keys = k_buf[block].reshape(GROUP * seq, dim)
            values = v_buf[block].reshape(GROUP * seq, dim)
            scores = lax.dot_general(query, keys, (((1,), (1,)), ((), ())), preferred_element_type=jnp.float32) * (dim ** -0.5)
            scores = jnp.where((col >= first_col) & (col <= last_col), scores, -jnp.inf)
            weight = jnp.exp(scores - jnp.max(scores, axis=-1, keepdims=True))
            prob = (weight * (1.0 / jnp.sum(weight, axis=-1, keepdims=True))).astype(jnp.bfloat16)
            done.append((block, jnp.dot(prob, values, preferred_element_type=jnp.float32)))
        for block, mixed in done:
            for j in range(heads):
                mix_buf[block, pl.ds(j * dim, dim)] = mixed[j * GROUP:(j + 1) * GROUP]
        return carry

    lax.fori_loop(0, groups // TOGETHER, attend, 0)
    out_ref[...] = mix_buf[...].astype(jnp.bfloat16)

    def drain(g, carry):
        for copy in store(g):
            copy.wait()
        return carry

    lax.fori_loop(0, groups, drain, 0)


CHUNKS = 4
GROUP = 8
ROWS = 16
TOGETHER = 4


def attention_call(layer, x, norm, positions, freqs, w_query, w_key, w_value, k_cache, v_cache, k_done, v_done):
    rows, width = x.shape
    inner = w_query.shape[2]
    seq, dim = k_cache.shape[2], k_cache.shape[3]
    bf16 = jnp.bfloat16
    first = k_done is None
    vmem = pl.BlockSpec(memory_space=pltpu.VMEM)
    hbm = pl.BlockSpec(memory_space=pltpu.HBM)
    smem = pl.BlockSpec(memory_space=pltpu.SMEM)
    args = [x, norm, positions, positions[None, :], freqs, w_query, w_key, w_value, k_cache, v_cache]
    specs = [vmem, vmem, smem, vmem, vmem, hbm, hbm, hbm, hbm, hbm]
    aliases = {}
    if not first:
        aliases = {len(args): 1, len(args) + 1: 2}
        args += [k_done, v_done]
        specs += [hbm, hbm]
    weights = width * (inner + 2 * dim)
    return pl.pallas_call(
        functools.partial(attention_kernel, layer, first),
        out_shape=[jax.ShapeDtypeStruct((rows, inner), bf16), jax.ShapeDtypeStruct(k_cache.shape, bf16), jax.ShapeDtypeStruct(v_cache.shape, bf16)],
        in_specs=specs,
        out_specs=[vmem, hbm, hbm],
        scratch_shapes=[
            pltpu.VMEM((width, inner), bf16),
            pltpu.VMEM((width, 2 * dim), bf16),
            pltpu.VMEM((rows, seq, dim), bf16),
            pltpu.VMEM((rows, seq, dim), bf16),
            pltpu.VMEM((rows, width), bf16),
            pltpu.VMEM((rows, inner), jnp.float32),
            pltpu.VMEM((rows, 2 * dim), jnp.float32),
            pltpu.VMEM((rows, inner), jnp.float32),
            pltpu.SemaphoreType.DMA((3, CHUNKS)),
            pltpu.SemaphoreType.DMA((2,)),
            pltpu.SemaphoreType.DMA((2, rows // GROUP)),
        ],
        input_output_aliases=aliases,
        compiler_params=pltpu.CompilerParams(vmem_limit_bytes=67043328),
        cost_estimate=pl.CostEstimate(flops=2 * rows * weights, bytes_accessed=2 * weights, transcendentals=rows * seq),
        name='attention_layer',
    )(*args)


PIECES = 5
TILE = 256


def mlp_kernel(layer, chips, attn_ref, res_ref, norm_ref, wo_hbm, wg_hbm, wu_hbm, wd_hbm, out_ref,
               o_buf, g_buf, u_buf, d_buf, full, part, act, res, swap_in, summed, owner_in,
               w_sem, io_sem, rs_send, rs_recv, ag_send, ag_recv):
    rows, width = full.shape
    piece = width // PIECES
    half_rows = rows // 2
    own_rows = half_rows // chips
    me = lax.axis_index('tp')
    core = lax.rem(me, 2)
    chip = me // 2
    partner = me + 1 - 2 * core
    peers = [2 * lax.rem(chip + hop, chips) + core for hop in range(chips)]
    hops = tuple(sorted(range(1, chips), key=lambda hop: -min(hop, chips - hop)))
    nearest = hops[::-1]
    n_gate = g_buf.shape[0]

    def piece_cols(p):
        return pl.ds(p * piece, piece)

    def rows_of(offset):
        return pl.ds(pl.multiple_of(core * half_rows + lax.rem(chip + offset, chips) * own_rows, own_rows), own_rows)

    def block(offset):
        return pl.ds(pl.multiple_of(lax.rem(chip + offset, chips) * own_rows, own_rows), own_rows)

    mine = rows_of(0)
    other_rows = pl.ds(pl.multiple_of((1 - core) * half_rows, half_rows), half_rows)
    my_rows = pl.ds(pl.multiple_of(core * half_rows, half_rows), half_rows)

    def load_out(p):
        return pltpu.make_async_copy(wo_hbm.at[layer, :, piece_cols(p)], o_buf.at[p], w_sem.at[p])

    def load_down(p):
        return pltpu.make_async_copy(wd_hbm.at[layer, :, piece_cols(p)], d_buf.at[p], w_sem.at[PIECES + p])

    def load_gate(j):
        cols = pl.ds(pl.multiple_of(j * TILE, TILE), TILE)
        return pltpu.make_async_copy(wg_hbm.at[layer, :, cols], g_buf.at[j], w_sem.at[2 * PIECES + j])

    def load_up(j):
        cols = pl.ds(pl.multiple_of(j * TILE, TILE), TILE)
        return pltpu.make_async_copy(wu_hbm.at[layer, :, cols], u_buf.at[j], w_sem.at[2 * PIECES + n_gate + j])

    load_res = pltpu.make_async_copy(res_ref.at[mine], res, io_sem.at[0])

    def store(p):
        return pltpu.make_async_copy(full.at[:, piece_cols(p)], out_ref.at[:, piece_cols(p)], io_sem.at[1 + p])

    for p in range(PIECES):
        load_out(p).start()
    load_res.start()

    def start_gate_up():
        for j in range(n_gate):
            load_gate(j).start()
            load_up(j).start()

    def start_down():
        for p in range(PIECES):
            load_down(p).start()

    barrier = pltpu.get_barrier_semaphore()
    for peer in [partner] + peers[1:]:
        pl.semaphore_signal(barrier, inc=1, device_id={'tp': peer}, device_id_type=pl.DeviceIdType.MESH)
    pl.semaphore_wait(barrier, chips)

    def remote(src, dst, send_sem, recv_sem, peer):
        return pltpu.make_async_remote_copy(src_ref=src, dst_ref=dst, send_sem=send_sem, recv_sem=recv_sem, device_id={'tp': peer}, device_id_type=pl.DeviceIdType.MESH)

    def swap(p):
        return remote(part.at[other_rows, piece_cols(p)], swap_in.at[p], rs_send.at[0, p], rs_recv.at[0, p], partner)

    def to_owner(p, hop):
        return remote(summed.at[p, block(hop)], owner_in.at[hop - 1, p], rs_send.at[hop, p], rs_recv.at[hop, p], peers[hop])

    def spread(p, hop):
        return remote(res.at[:, piece_cols(p)], full.at[mine, piece_cols(p)], ag_send.at[hop, p], ag_recv.at[hop, p], peers[hop] if hop else partner)

    def forward(p, hop):
        landed = full.at[rows_of(chips - hop), piece_cols(p)]
        return remote(landed, landed, ag_send.at[chips + hop - 1, p], ag_recv.at[chips + hop - 1, p], partner)

    def add_over_tp(lhs_ref, w_buf, load, after_products, after_sums):
        def product(p):
            load(p).wait()
            for i in range(piece // TILE):
                part[:, pl.ds(p * piece + i * TILE, TILE)] = jnp.dot(
                    lhs_ref[...], w_buf[p, :, pl.ds(i * TILE, TILE)], preferred_element_type=jnp.float32).astype(jnp.bfloat16)
            swap(p).start()

        def chip_sum(p):
            swap(p).wait_recv()
            summed[p] = (part[my_rows, piece_cols(p)].astype(jnp.float32) + swap_in[p].astype(jnp.float32)).astype(jnp.bfloat16)
            for hop in hops:
                to_owner(p, hop).start()

        product(0)
        for p in range(1, PIECES):
            product(p)
            chip_sum(p - 1)
        after_products()
        chip_sum(PIECES - 1)
        after_sums()
        for p in range(PIECES):
            total = summed[p, block(0)].astype(jnp.float32)
            for hop in range(1, chips):
                to_owner(p, hop).wait_recv()
                total = total + owner_in[hop - 1, p].astype(jnp.float32)
            new = res[:, piece_cols(p)].astype(jnp.float32) + total.astype(jnp.bfloat16).astype(jnp.float32)
            new = new.astype(jnp.bfloat16)
            res[:, piece_cols(p)] = new
            full[mine, piece_cols(p)] = new
            for hop in hops + (0,):
                spread(p, hop).start()
        for p in range(PIECES):
            for hop in nearest:
                spread(p, hop).wait_recv()
                forward(p, hop).start()

    def gathered(p):
        spread(p, 0).wait_recv()
        for hop in nearest:
            forward(p, hop).wait_recv()

    def drain_sends():
        for p in range(PIECES):
            swap(p).wait_send()
            for hop in range(1, chips):
                to_owner(p, hop).wait_send()
                forward(p, hop).wait_send()
            for hop in range(chips):
                spread(p, hop).wait_send()

    load_res.wait()
    add_over_tp(attn_ref, o_buf, load_out, start_gate_up, start_down)
    sum_sq = jnp.zeros((rows, 1), jnp.float32)
    for p in range(PIECES):
        gathered(p)
        new = full[:, piece_cols(p)].astype(jnp.float32)
        sum_sq = sum_sq + jnp.sum(new * new, axis=-1, keepdims=True)
    drain_sends()
    scale = lax.rsqrt(sum_sq / width + 1e-5)
    for p in range(PIECES):
        cols = piece_cols(p)
        part[:, cols] = (full[:, cols].astype(jnp.float32) * scale * norm_ref[layer:layer + 1, cols].astype(jnp.float32)).astype(jnp.bfloat16)

    def gate_up(j, carry):
        load_gate(j).wait()
        load_up(j).wait()
        gate = jnp.dot(part[...], g_buf[j], preferred_element_type=jnp.float32).astype(jnp.bfloat16).astype(jnp.float32)
        up = jnp.dot(part[...], u_buf[j], preferred_element_type=jnp.float32).astype(jnp.bfloat16).astype(jnp.float32)
        act[:, pl.ds(pl.multiple_of(j * TILE, TILE), TILE)] = (gate * jax.nn.sigmoid(gate) * up).astype(jnp.bfloat16)
        return carry

    lax.fori_loop(0, n_gate, gate_up, 0)
    add_over_tp(act, d_buf, load_down, lambda: None, lambda: None)
    for p in range(PIECES):
        gathered(p)
        store(p).start()
    drain_sends()
    for p in range(PIECES):
        store(p).wait()


def mlp_call(layer, chips, attended, hidden, norm, w_out, w_gate, w_up, w_down):
    rows, inner = attended.shape
    width = w_gate.shape[1]
    ff = w_gate.shape[2]
    piece = width // PIECES
    own_rows = rows // 2 // chips
    bf16 = jnp.bfloat16
    vmem = pl.BlockSpec(memory_space=pltpu.VMEM)
    hbm = pl.BlockSpec(memory_space=pltpu.HBM)
    scratch = [
        pltpu.VMEM((PIECES, inner, piece), bf16),
        pltpu.VMEM((ff // TILE, width, TILE), bf16),
        pltpu.VMEM((ff // TILE, width, TILE), bf16),
        pltpu.VMEM((PIECES, ff, piece), bf16),
        pltpu.VMEM((rows, width), bf16),
        pltpu.VMEM((rows, width), bf16),
        pltpu.VMEM((rows, ff), bf16),
        pltpu.VMEM((own_rows, width), bf16),
        pltpu.VMEM((PIECES, rows // 2, piece), bf16),
        pltpu.VMEM((PIECES, rows // 2, piece), bf16),
        pltpu.VMEM((chips - 1, PIECES, own_rows, piece), bf16),
        pltpu.SemaphoreType.DMA((2 * PIECES + 2 * (ff // TILE),)),
        pltpu.SemaphoreType.DMA((1 + PIECES,)),
        pltpu.SemaphoreType.DMA((chips, PIECES)),
        pltpu.SemaphoreType.DMA((chips, PIECES)),
        pltpu.SemaphoreType.DMA((2 * chips - 1, PIECES)),
        pltpu.SemaphoreType.DMA((2 * chips - 1, PIECES)),
    ]
    weights = inner * width + 3 * width * ff
    return pl.pallas_call(
        functools.partial(mlp_kernel, layer, chips),
        out_shape=jax.ShapeDtypeStruct((rows, width), bf16),
        in_specs=[vmem, hbm, vmem, hbm, hbm, hbm, hbm],
        out_specs=hbm,
        scratch_shapes=scratch,
        compiler_params=pltpu.CompilerParams(collective_id=layer, has_side_effects=True, vmem_limit_bytes=67043328),
        cost_estimate=pl.CostEstimate(flops=2 * rows * weights, bytes_accessed=2 * weights, transcendentals=rows * ff),
        name='mlp_layer',
    )(attended, hidden, norm, w_out, w_gate, w_up, w_down)


def solution(mesh):
    row_spec = P('dp', None)
    pos_spec = P('dp')
    cache_spec = P(None, 'dp', None, 'tp', None)
    norm_spec = P(None, None)
    col_spec = P(None, None, 'tp')
    split_rows = P(None, 'tp', None)
    chips = mesh.shape['tp'] // 2

    def local_step(hidden, positions, k_cache, v_cache, attn_norm, w_query, w_key, w_value, w_out, mlp_norm, w_gate, w_up, w_down):
        layers, batch, seq, kv_heads, dim = k_cache.shape
        freqs = rope_freqs(dim)
        k_old = k_cache.reshape(layers, batch, seq, dim)
        v_old = v_cache.reshape(layers, batch, seq, dim)
        k_out = v_out = None
        for layer in range(layers):
            attended, k_out, v_out = attention_call(layer, hidden, attn_norm, positions, freqs, w_query, w_key, w_value, k_old, v_old, k_out, v_out)
            hidden = mlp_call(layer, chips, attended, hidden, mlp_norm, w_out, w_gate, w_up, w_down)
        shape = (layers, batch, seq, kv_heads, dim)
        return hidden, k_out.reshape(shape), v_out.reshape(shape)

    return jax.shard_map(local_step, mesh=mesh, in_specs=(row_spec, pos_spec, cache_spec, cache_spec, norm_spec, col_spec, col_spec, col_spec, split_rows, norm_spec, col_spec, col_spec, split_rows), out_specs=(row_spec, cache_spec, cache_spec), check_vma=False)
```

time: 153 us -> 135 us (0.88)
  Pallas kernels: 145 us -> 131 us
  local copies, waits for them, and re-layouts: 5.35 us -> 2.46 us
    pallas_call x2, Pallas kernels: 114 us -> 103 us  [mlp_call(): pl.pallas_call(functools.partial(mlp_kernel, layer, chips), out_shape=jax...]
    pallas_call x2, Pallas kernels: 30.9 us -> 27.9 us  [attention_call(): pl.pallas_call(functools.partial(attention_kernel, layer, first), out_sha...]
where the time goes in v3:
time: 135 us; the launch traced here: 134 us
  Pallas kernels  131 us (97%)
  local copies, waits for them, and re-layouts  2.46 us (2%)
    pallas_call x2, Pallas kernels, mlp_call(): pl.pallas_call(functools.partial(mlp_kernel, layer, chips), out_shape=jax...  103 us
    pallas_call x2, Pallas kernels, attention_call(): pl.pallas_call(functools.partial(attention_kernel, layer, first), out_sha...  27.9 us

profile of v3, /device:TPU:113, one launch (start us, length us, event | category | flops | bytes accessed | tf_op | source)
XLA Modules:
  0.0 134.4 jit_solution(3747099537767543953)
XLA Ops:
  0.7 0.7 maximum_bitcast_fusion.freq_ref
  1.3 14.0 %attention_layer.2 = (bf16[128,512]{1,0:T(8,128)(2,1)}, bf16[2,128,64,128]{3,2,1,0:T(8,128)(2,1)}, bf16[2,128,64,128]{3,2,1,0:T(8,128)(2,1)}) custom-call(bf16[128,5120]{1,0:T(8,128)(2,1)} %res_ref.1, bf16[2,5120]{1,0:T(2,128)(2,1)} %norm_ref.6, s32[128]{0:T(128)} %pos_smem.3, s32[1,128]{1,0:T(1,128)} %bitcast.17, f32[1,128]{1,0:T(1,128)} %maximum_bitcast_fusion.freq_ref, ...), custom_call_target="tpu_custom_call" | custom-call | flops 1006632960 | bytes 7864320 | tf_op jit(solution)/shard_map/attention_layer/pallas_call | solution.py:180
  15.3 52.7 %mlp_layer.2.x_ref.res_ref = bf16[128,5120]{1,0:T(8,128)(2,1)} custom-call(bf16[128,512]{1,0:T(8,128)(2,1)} %get-tuple-element.9.attn_ref, bf16[128,5120]{1,0:T(8,128)(2,1)} %res_ref.1, bf16[2,5120]{1,0:T(2,128)(2,1)} %norm_ref.7, bf16[2,512,5120]{2,1,0:T(8,128)(2,1)} %wo_hbm.3, bf16[2,5120,1792]{2,1,0:T(8,128)(2,1)} %wg_hbm.3, ...), custom_call_target="tpu_custom_call" | custom-call | flops 7717519360 | bytes 60293120 | tf_op jit(solution)/shard_map/mlp_layer/pallas_call | solution.py:402
  68.0 13.9 %attention_layer.3 = (bf16[128,512]{1,0:T(8,128)(2,1)}, bf16[2,128,64,128]{3,2,1,0:T(8,128)(2,1)}, bf16[2,128,64,128]{3,2,1,0:T(8,128)(2,1)}) custom-call(bf16[128,5120]{1,0:T(8,128)(2,1)} %mlp_layer.2.x_ref.res_ref, bf16[2,5120]{1,0:T(2,128)(2,1)} %norm_ref.6, s32[128]{0:T(128)} %pos_smem.3, ...), custom_call_target="tpu_custom_call", output_to_operand_aliasing={{1}: (10, {}), {2}: (11, {})} | custom-call | flops 1006632960 | bytes 7864320 | tf_op jit(solution)/shard_map/attention_layer/pallas_call | solution.py:180
  81.9 50.0 %mlp_layer.3 = bf16[128,5120]{1,0:T(8,128)(2,1)} custom-call(bf16[128,512]{1,0:T(8,128)(2,1)} %get-tuple-element.12.attn_ref, bf16[128,5120]{1,0:T(8,128)(2,1)} %mlp_layer.2.x_ref.res_ref, bf16[2,5120]{1,0:T(2,128)(2,1)} %norm_ref.7, bf16[2,512,5120]{2,1,0:T(8,128)(2,1)} %wo_hbm.3, bf16[2,5120,1792]{2,1,0:T(8,128)(2,1)} %wg_hbm.3, ...), custom_call_target="tpu_custom_call" | custom-call | flops 7717519360 | bytes 60293120 | tf_op jit(solution)/shard_map/mlp_layer/pallas_call | solution.py:402
  131.9 2.5 %copy.23 = bf16[128,5120]{1,0:T(8,128)(2,1)} copy(bf16[128,5120]{1,0:T(8,128)(2,1)} %mlp_layer.3) | data formatting | bytes 2621440
  (1 shorter events, 0.0 us)

commit v4 on v3

--- a/solution.py
+++ b/solution.py
@@ -2,6 +2,7 @@
 import math
 import jax
 import jax.numpy as jnp
+import numpy as np
 from jax import lax
 from jax.experimental import pallas as pl
 from jax.experimental.pallas import tpu as pltpu
@@ -10,18 +11,18 @@
 
 def rope_freqs(head_dim):
     half_dim = head_dim // 2
-    inv_freq = jnp.power(500000.0, -jnp.arange(half_dim, dtype=jnp.float32) * (2.0 / head_dim))
+    inv_freq = np.power(np.float64(500000.0), -np.arange(half_dim) * (2.0 / head_dim))
     wavelen = (2.0 * math.pi) / inv_freq
     smooth = (8192.0 / wavelen - 1.0) / 3.0
     blended = (1.0 - smooth) * inv_freq / 8.0 + smooth * inv_freq
-    scaled = jnp.where(wavelen < 2048.0, inv_freq, jnp.where(wavelen > 8192.0, inv_freq / 8.0, blended))
-    return jnp.concatenate([scaled, scaled])[None, :]
+    scaled = np.where(wavelen < 2048.0, inv_freq, np.where(wavelen > 8192.0, inv_freq / 8.0, blended))
+    return np.concatenate([scaled, scaled])[None, :].astype(np.float32)
 
 
 def attention_kernel(layer, first, x_ref, norm_ref, pos_smem, pos_ref, freq_ref, wq_hbm, wk_hbm, wv_hbm, k_hbm, v_hbm, *rest):
     if not first:
         rest = rest[2:]
-    (out_ref, k_out, v_out, wq_buf, wkv_buf, k_buf, v_buf, h_buf, q_buf, kv_buf, mix_buf, w_sem, in_sem, out_sem) = rest
+    (out_ref, k_out, v_out, wq_buf, wkv_buf, k_buf, v_buf, h_buf, q_buf, kv_buf, mix_buf, prob_buf, att_buf, x_buf, norm_buf, w_sem, in_sem, out_sem) = rest
     rows, width = x_ref.shape
     inner = wq_buf.shape[1]
     seq, dim = k_buf.shape[1], k_buf.shape[2]
@@ -37,20 +38,26 @@
 
     load_k = pltpu.make_async_copy(k_hbm.at[layer], k_buf, in_sem.at[0])
     load_v = pltpu.make_async_copy(v_hbm.at[layer], v_buf, in_sem.at[1])
+    load_x = pltpu.make_async_copy(x_ref, x_buf, in_sem.at[3])
+    load_norm = pltpu.make_async_copy(norm_ref, norm_buf, in_sem.at[4])
+    load_x.start()
+    load_norm.start()
     for i in range(CHUNKS):
         for copy in load_weights(i):
             copy.start()
     load_k.start()
     load_v.start()
 
+    load_x.wait()
+    load_norm.wait()
     sum_sq = jnp.zeros((rows, 1), jnp.float32)
     for i in range(CHUNKS):
-        part = x_ref[:, pl.ds(i * chunk, chunk)].astype(jnp.float32)
+        part = x_buf[:, pl.ds(i * chunk, chunk)].astype(jnp.float32)
         sum_sq = sum_sq + jnp.sum(part * part, axis=-1, keepdims=True)
     scale = lax.rsqrt(sum_sq / width + 1e-5)
     for i in range(CHUNKS):
         cols = pl.ds(i * chunk, chunk)
-        h_buf[:, cols] = (x_ref[:, cols].astype(jnp.float32) * scale * norm_ref[layer:layer + 1, cols].astype(jnp.float32)).astype(jnp.bfloat16)
+        h_buf[:, cols] = (x_buf[:, cols].astype(jnp.float32) * scale * norm_buf[layer:layer + 1, cols].astype(jnp.float32)).astype(jnp.bfloat16)
 
     square = (rows, rows)
     diagonal = lax.broadcasted_iota(jnp.int32, square, 0) == lax.broadcasted_iota(jnp.int32, square, 1)
@@ -122,29 +129,42 @@
     first_col = request * seq
     col = lax.broadcasted_iota(jnp.int32, (heads * GROUP, GROUP * seq), 1)
 
-    def attend(step, carry):
+    def weigh(step, carry):
         done = []
         for k in range(TOGETHER):
-            base = pl.multiple_of((step * TOGETHER + k) * GROUP, GROUP)
+            g = step * TOGETHER + k
+            base = pl.multiple_of(g * GROUP, GROUP)
             block = pl.ds(base, GROUP)
             last_col = first_col
             for i in range(GROUP):
                 last_col = jnp.where(request == i, i * seq + pos_smem[base + i], last_col)
             query = jnp.concatenate([q_buf[block, pl.ds(j * dim, dim)] for j in range(heads)], axis=0).astype(jnp.bfloat16)
             keys = k_buf[block].reshape(GROUP * seq, dim)
-            values = v_buf[block].reshape(GROUP * seq, dim)
             scores = lax.dot_general(query, keys, (((1,), (1,)), ((), ())), preferred_element_type=jnp.float32) * (dim ** -0.5)
             scores = jnp.where((col >= first_col) & (col <= last_col), scores, -jnp.inf)
             weight = jnp.exp(scores - jnp.max(scores, axis=-1, keepdims=True))
-            prob = (weight * (1.0 / jnp.sum(weight, axis=-1, keepdims=True))).astype(jnp.bfloat16)
-            done.append((block, jnp.dot(prob, values, preferred_element_type=jnp.float32)))
+            done.append((g, (weight * (1.0 / jnp.sum(weight, axis=-1, keepdims=True))).astype(jnp.bfloat16)))
+        for g, prob in done:
+            prob_buf[g] = prob
+        return carry
+
+    def mix(step, carry):
+        done = []
+        for k in range(TOGETHER):
+            g = step * TOGETHER + k
+            block = pl.ds(pl.multiple_of(g * GROUP, GROUP), GROUP)
+            values = v_buf[block].reshape(GROUP * seq, dim)
+            done.append((block, jnp.dot(prob_buf[g], values, preferred_element_type=jnp.float32)))
         for block, mixed in done:
             for j in range(heads):
                 mix_buf[block, pl.ds(j * dim, dim)] = mixed[j * GROUP:(j + 1) * GROUP]
         return carry
 
-    lax.fori_loop(0, groups // TOGETHER, attend, 0)
-    out_ref[...] = mix_buf[...].astype(jnp.bfloat16)
+    lax.fori_loop(0, groups // TOGETHER, weigh, 0)
+    lax.fori_loop(0, groups // TOGETHER, mix, 0)
+    att_buf[...] = mix_buf[...].astype(jnp.bfloat16)
+    store_out = pltpu.make_async_copy(att_buf, out_ref, in_sem.at[2])
+    store_out.start()
 
     def drain(g, carry):
         for copy in store(g):
@@ -152,6 +172,7 @@
         return carry
 
     lax.fori_loop(0, groups, drain, 0)
+    store_out.wait()
 
 
 CHUNKS = 4
@@ -170,7 +191,7 @@
     hbm = pl.BlockSpec(memory_space=pltpu.HBM)
     smem = pl.BlockSpec(memory_space=pltpu.SMEM)
     args = [x, norm, positions, positions[None, :], freqs, w_query, w_key, w_value, k_cache, v_cache]
-    specs = [vmem, vmem, smem, vmem, vmem, hbm, hbm, hbm, hbm, hbm]
+    specs = [hbm, hbm, smem, vmem, vmem, hbm, hbm, hbm, hbm, hbm]
     aliases = {}
     if not first:
         aliases = {len(args): 1, len(args) + 1: 2}
@@ -181,7 +202,7 @@
         functools.partial(attention_kernel, layer, first),
         out_shape=[jax.ShapeDtypeStruct((rows, inner), bf16), jax.ShapeDtypeStruct(k_cache.shape, bf16), jax.ShapeDtypeStruct(v_cache.shape, bf16)],
         in_specs=specs,
-        out_specs=[vmem, hbm, hbm],
+        out_specs=[hbm, hbm, hbm],
         scratch_shapes=[
             pltpu.VMEM((width, inner), bf16),
             pltpu.VMEM((width, 2 * dim), bf16),
@@ -191,8 +212,12 @@
             pltpu.VMEM((rows, inner), jnp.float32),
             pltpu.VMEM((rows, 2 * dim), jnp.float32),
             pltpu.VMEM((rows, inner), jnp.float32),
+            pltpu.VMEM((rows // GROUP, GROUP * inner // dim, GROUP * seq), bf16),
+            pltpu.VMEM((rows, inner), bf16),
+            pltpu.VMEM((rows, width), bf16),
+            pltpu.VMEM(norm.shape, bf16),
             pltpu.SemaphoreType.DMA((3, CHUNKS)),
-            pltpu.SemaphoreType.DMA((2,)),
+            pltpu.SemaphoreType.DMA((5,)),
             pltpu.SemaphoreType.DMA((2, rows // GROUP)),
         ],
         input_output_aliases=aliases,
@@ -206,8 +231,8 @@
 TILE = 256
 
 
-def mlp_kernel(layer, chips, attn_ref, res_ref, norm_ref, wo_hbm, wg_hbm, wu_hbm, wd_hbm, out_ref,
-               o_buf, g_buf, u_buf, d_buf, full, part, act, res, swap_in, summed, owner_in,
+def mlp_kernel(layer, chips, attn_hbm, res_ref, norm_hbm, wo_hbm, wg_hbm, wu_hbm, wd_hbm, out_ref,
+               o_buf, g_buf, u_buf, d_buf, full, part, act, res, attn_ref, norm_ref, swap_in, summed, owner_in,
                w_sem, io_sem, rs_send, rs_recv, ag_send, ag_recv):
     rows, width = full.shape
     piece = width // PIECES
@@ -250,13 +275,17 @@
         return pltpu.make_async_copy(wu_hbm.at[layer, :, cols], u_buf.at[j], w_sem.at[2 * PIECES + n_gate + j])
 
     load_res = pltpu.make_async_copy(res_ref.at[mine], res, io_sem.at[0])
+    load_attn = pltpu.make_async_copy(attn_hbm, attn_ref, io_sem.at[1 + PIECES])
+    load_norm = pltpu.make_async_copy(norm_hbm, norm_ref, io_sem.at[2 + PIECES])
 
     def store(p):
         return pltpu.make_async_copy(full.at[:, piece_cols(p)], out_ref.at[:, piece_cols(p)], io_sem.at[1 + p])
 
+    load_attn.start()
     for p in range(PIECES):
         load_out(p).start()
     load_res.start()
+    load_norm.start()
 
     def start_gate_up():
         for j in range(n_gate):
@@ -339,7 +368,9 @@
             for hop in range(chips):
                 spread(p, hop).wait_send()
 
+    load_attn.wait()
     load_res.wait()
+    load_norm.wait()
     add_over_tp(attn_ref, o_buf, load_out, start_gate_up, start_down)
     sum_sq = jnp.zeros((rows, 1), jnp.float32)
     for p in range(PIECES):
@@ -377,7 +408,6 @@
     piece = width // PIECES
     own_rows = rows // 2 // chips
     bf16 = jnp.bfloat16
-    vmem = pl.BlockSpec(memory_space=pltpu.VMEM)
     hbm = pl.BlockSpec(memory_space=pltpu.HBM)
     scratch = [
         pltpu.VMEM((PIECES, inner, piece), bf16),
@@ -388,11 +418,13 @@
         pltpu.VMEM((rows, width), bf16),
         pltpu.VMEM((rows, ff), bf16),
         pltpu.VMEM((own_rows, width), bf16),
+        pltpu.VMEM((rows, inner), bf16),
+        pltpu.VMEM(norm.shape, bf16),
         pltpu.VMEM((PIECES, rows // 2, piece), bf16),
         pltpu.VMEM((PIECES, rows // 2, piece), bf16),
         pltpu.VMEM((chips - 1, PIECES, own_rows, piece), bf16),
         pltpu.SemaphoreType.DMA((2 * PIECES + 2 * (ff // TILE),)),
-        pltpu.SemaphoreType.DMA((1 + PIECES,)),
+        pltpu.SemaphoreType.DMA((3 + PIECES,)),
         pltpu.SemaphoreType.DMA((chips, PIECES)),
         pltpu.SemaphoreType.DMA((chips, PIECES)),
         pltpu.SemaphoreType.DMA((2 * chips - 1, PIECES)),
@@ -402,7 +434,7 @@
     return pl.pallas_call(
         functools.partial(mlp_kernel, layer, chips),
         out_shape=jax.ShapeDtypeStruct((rows, width), bf16),
-        in_specs=[vmem, hbm, vmem, hbm, hbm, hbm, hbm],
+        in_specs=[hbm] * 7,
         out_specs=hbm,
         scratch_shapes=scratch,
         compiler_params=pltpu.CompilerParams(collective_id=layer, has_side_effects=True, vmem_limit_bytes=67043328),

time: 135 us -> 127 us (0.941)
  Pallas kernels: 131 us -> 124 us
    pallas_call x2, Pallas kernels: 27.9 us -> 22.9 us  [attention_call(): pl.pallas_call(functools.partial(attention_kernel, layer, first), out_sha...]
    pallas_call x2, Pallas kernels: 103 us -> 101 us  [mlp_call(): pl.pallas_call(functools.partial(mlp_kernel, layer, chips), out_shape=jax...]
where the time goes in v4:
time: 127 us
  Pallas kernels  124 us (98%)
  local copies, waits for them, and re-layouts  2.46 us (2%)
    pallas_call x2, Pallas kernels, mlp_call(): pl.pallas_call(functools.partial(mlp_kernel, layer, chips), out_shape=jax...  101 us
    pallas_call x2, Pallas kernels, attention_call(): pl.pallas_call(functools.partial(attention_kernel, layer, first), out_sha...  22.9 us

profile of v4, /device:TPU:113, one launch (start us, length us, event | category | flops | bytes accessed | tf_op | source)
XLA Modules:
  0.0 126.6 jit_solution(9329434840787828617)
XLA Ops:
  0.6 11.6 %attention_layer.2 = (bf16[128,512]{1,0:T(8,128)(2,1)}, bf16[2,128,64,128]{3,2,1,0:T(8,128)(2,1)}, bf16[2,128,64,128]{3,2,1,0:T(8,128)(2,1)}) custom-call(bf16[128,5120]{1,0:T(8,128)(2,1)} %res_ref.1, bf16[2,5120]{1,0:T(2,128)(2,1)} %norm_ref.3, s32[128]{0:T(128)} %pos_smem.3, s32[1,128]{1,0:T(1,128)} %bitcast.15, f32[1,128]{1,0:T(1,128)} %constant.2.clone.freq_ref, ...), custom_call_target="tpu_custom_call" | custom-call | flops 1006632960 | bytes 7864320 | tf_op jit(solution)/shard_map/attention_layer/pallas_call | solution.py:201
  12.2 51.7 %mlp_layer.2.x_ref.res_ref = bf16[128,5120]{1,0:T(8,128)(2,1)} custom-call(bf16[128,512]{1,0:T(8,128)(2,1)} %get-tuple-element.9.attn_hbm, bf16[128,5120]{1,0:T(8,128)(2,1)} %res_ref.1, bf16[2,5120]{1,0:T(2,128)(2,1)} %norm_hbm.3, bf16[2,512,5120]{2,1,0:T(8,128)(2,1)} %wo_hbm.3, bf16[2,5120,1792]{2,1,0:T(8,128)(2,1)} %wg_hbm.3, ...), custom_call_target="tpu_custom_call" | custom-call | flops 7717519360 | bytes 60293120 | tf_op jit(solution)/shard_map/mlp_layer/pallas_call | solution.py:434
  63.9 11.4 %attention_layer.3 = (bf16[128,512]{1,0:T(8,128)(2,1)}, bf16[2,128,64,128]{3,2,1,0:T(8,128)(2,1)}, bf16[2,128,64,128]{3,2,1,0:T(8,128)(2,1)}) custom-call(bf16[128,5120]{1,0:T(8,128)(2,1)} %mlp_layer.2.x_ref.res_ref, bf16[2,5120]{1,0:T(2,128)(2,1)} %norm_ref.3, s32[128]{0:T(128)} %pos_smem.3, ...), custom_call_target="tpu_custom_call", output_to_operand_aliasing={{1}: (10, {}), {2}: (11, {})} | custom-call | flops 1006632960 | bytes 7864320 | tf_op jit(solution)/shard_map/attention_layer/pallas_call | solution.py:201
  75.3 48.8 %mlp_layer.3 = bf16[128,5120]{1,0:T(8,128)(2,1)} custom-call(bf16[128,512]{1,0:T(8,128)(2,1)} %get-tuple-element.12.attn_hbm, bf16[128,5120]{1,0:T(8,128)(2,1)} %mlp_layer.2.x_ref.res_ref, bf16[2,5120]{1,0:T(2,128)(2,1)} %norm_hbm.3, bf16[2,512,5120]{2,1,0:T(8,128)(2,1)} %wo_hbm.3, bf16[2,5120,1792]{2,1,0:T(8,128)(2,1)} %wg_hbm.3, ...), custom_call_target="tpu_custom_call" | custom-call | flops 7717519360 | bytes 60293120 | tf_op jit(solution)/shard_map/mlp_layer/pallas_call | solution.py:434
  124.2 2.5 %copy.24 = bf16[128,5120]{1,0:T(8,128)(2,1)} copy(bf16[128,5120]{1,0:T(8,128)(2,1)} %mlp_layer.3) | data formatting | bytes 2621440

commit v5 on v4

--- a/solution.py
+++ b/solution.py
@@ -175,10 +175,10 @@
     store_out.wait()
 
 
-CHUNKS = 4
+CHUNKS = 2
 GROUP = 8
 ROWS = 16
-TOGETHER = 4
+TOGETHER = 16
 
 
 def attention_call(layer, x, norm, positions, freqs, w_query, w_key, w_value, k_cache, v_cache, k_done, v_done):
@@ -228,6 +228,7 @@
 
 
 PIECES = 5
+RELAYED = 4
 TILE = 256
 
 
@@ -245,6 +246,7 @@
     peers = [2 * lax.rem(chip + hop, chips) + core for hop in range(chips)]
     hops = tuple(sorted(range(1, chips), key=lambda hop: -min(hop, chips - hop)))
     nearest = hops[::-1]
+    far = chips // 2
     n_gate = g_buf.shape[0]
 
     def piece_cols(p):
@@ -282,8 +284,7 @@
         return pltpu.make_async_copy(full.at[:, piece_cols(p)], out_ref.at[:, piece_cols(p)], io_sem.at[1 + p])
 
     load_attn.start()
-    for p in range(PIECES):
-        load_out(p).start()
+    load_out(0).start()
     load_res.start()
     load_norm.start()
 
@@ -300,6 +301,8 @@
     for peer in [partner] + peers[1:]:
         pl.semaphore_signal(barrier, inc=1, device_id={'tp': peer}, device_id_type=pl.DeviceIdType.MESH)
     pl.semaphore_wait(barrier, chips)
+    for p in range(1, PIECES):
+        load_out(p).start()
 
     def remote(src, dst, send_sem, recv_sem, peer):
         return pltpu.make_async_remote_copy(src_ref=src, dst_ref=dst, send_sem=send_sem, recv_sem=recv_sem, device_id={'tp': peer}, device_id_type=pl.DeviceIdType.MESH)
@@ -311,7 +314,11 @@
         return remote(summed.at[p, block(hop)], owner_in.at[hop - 1, p], rs_send.at[hop, p], rs_recv.at[hop, p], peers[hop])
 
     def spread(p, hop):
-        return remote(res.at[:, piece_cols(p)], full.at[mine, piece_cols(p)], ag_send.at[hop, p], ag_recv.at[hop, p], peers[hop] if hop else partner)
+        sems = ag_send.at[hop, p], ag_recv.at[hop, p]
+        if hop == far and p < RELAYED:
+            landed = full.at[rows_of(chips - 1 if p % 2 == 0 else 1), piece_cols(p)]
+            return remote(landed, landed, *sems, peers[1 if p % 2 == 0 else chips - 1])
+        return remote(res.at[:, piece_cols(p)], full.at[mine, piece_cols(p)], *sems, peers[hop] if hop else partner)
 
     def forward(p, hop):
         landed = full.at[rows_of(chips - hop), piece_cols(p)]
@@ -348,11 +355,17 @@
             res[:, piece_cols(p)] = new
             full[mine, piece_cols(p)] = new
             for hop in hops + (0,):
-                spread(p, hop).start()
+                if hop != far or p >= RELAYED:
+                    spread(p, hop).start()
         for p in range(PIECES):
-            for hop in nearest:
+            for hop in nearest[:-1]:
                 spread(p, hop).wait_recv()
+                if p < RELAYED and hop == (1 if p % 2 == 0 else chips - 1):
+                    spread(p, far).start()
                 forward(p, hop).start()
+        for p in range(PIECES):
+            spread(p, far).wait_recv()
+            forward(p, far).start()
 
     def gathered(p):
         spread(p, 0).wait_recv()

time: 127 us -> 119 us (0.937)
  Pallas kernels: 124 us -> 116 us
    pallas_call x2, Pallas kernels: 22.9 us -> 19 us  [attention_call(): pl.pallas_call(functools.partial(attention_kernel, layer, first), out_sha...]
    pallas_call x2, Pallas kernels: 101 us -> 96.8 us  [mlp_call(): pl.pallas_call(functools.partial(mlp_kernel, layer, chips), out_shape=jax...]
where the time goes in v5:
time: 119 us
  Pallas kernels  116 us (97%)
  local copies, waits for them, and re-layouts  2.46 us (2%)
    pallas_call x2, Pallas kernels, mlp_call(): pl.pallas_call(functools.partial(mlp_kernel, layer, chips), out_shape=jax...  96.8 us
    pallas_call x2, Pallas kernels, attention_call(): pl.pallas_call(functools.partial(attention_kernel, layer, first), out_sha...  19 us
    unnamed x1, local copies, waits for them, and re-layouts  2.46 us

profile of v5, /device:TPU:113, one launch (start us, length us, event | category | flops | bytes accessed | tf_op | source)
XLA Modules:
  0.0 118.9 jit_solution(14673699983707924144)
XLA Ops:
  0.6 9.5 %attention_layer.2 = (bf16[128,512]{1,0:T(8,128)(2,1)}, bf16[2,128,64,128]{3,2,1,0:T(8,128)(2,1)}, bf16[2,128,64,128]{3,2,1,0:T(8,128)(2,1)}) custom-call(bf16[128,5120]{1,0:T(8,128)(2,1)} %res_ref.1, bf16[2,5120]{1,0:T(2,128)(2,1)} %norm_ref.3, s32[128]{0:T(128)} %pos_smem.3, s32[1,128]{1,0:T(1,128)} %bitcast.15, f32[1,128]{1,0:T(1,128)} %constant.2.clone.freq_ref, ...), custom_call_target="tpu_custom_call" | custom-call | flops 1006632960 | bytes 7864320 | tf_op jit(solution)/shard_map/attention_layer/pallas_call | solution.py:201
  10.1 49.9 %mlp_layer.2.x_ref.res_ref = bf16[128,5120]{1,0:T(8,128)(2,1)} custom-call(bf16[128,512]{1,0:T(8,128)(2,1)} %get-tuple-element.9.attn_hbm, bf16[128,5120]{1,0:T(8,128)(2,1)} %res_ref.1, bf16[2,5120]{1,0:T(2,128)(2,1)} %norm_hbm.3, bf16[2,512,5120]{2,1,0:T(8,128)(2,1)} %wo_hbm.3, bf16[2,5120,1792]{2,1,0:T(8,128)(2,1)} %wg_hbm.3, ...), custom_call_target="tpu_custom_call" | custom-call | flops 7717519360 | bytes 60293120 | tf_op jit(solution)/shard_map/mlp_layer/pallas_call | solution.py:447
  60.0 9.5 %attention_layer.3 = (bf16[128,512]{1,0:T(8,128)(2,1)}, bf16[2,128,64,128]{3,2,1,0:T(8,128)(2,1)}, bf16[2,128,64,128]{3,2,1,0:T(8,128)(2,1)}) custom-call(bf16[128,5120]{1,0:T(8,128)(2,1)} %mlp_layer.2.x_ref.res_ref, bf16[2,5120]{1,0:T(2,128)(2,1)} %norm_ref.3, s32[128]{0:T(128)} %pos_smem.3, ...), custom_call_target="tpu_custom_call", output_to_operand_aliasing={{1}: (10, {}), {2}: (11, {})} | custom-call | flops 1006632960 | bytes 7864320 | tf_op jit(solution)/shard_map/attention_layer/pallas_call | solution.py:201
  69.5 46.9 %mlp_layer.3 = bf16[128,5120]{1,0:T(8,128)(2,1)} custom-call(bf16[128,512]{1,0:T(8,128)(2,1)} %get-tuple-element.12.attn_hbm, bf16[128,5120]{1,0:T(8,128)(2,1)} %mlp_layer.2.x_ref.res_ref, bf16[2,5120]{1,0:T(2,128)(2,1)} %norm_hbm.3, bf16[2,512,5120]{2,1,0:T(8,128)(2,1)} %wo_hbm.3, bf16[2,5120,1792]{2,1,0:T(8,128)(2,1)} %wg_hbm.3, ...), custom_call_target="tpu_custom_call" | custom-call | flops 7717519360 | bytes 60293120 | tf_op jit(solution)/shard_map/mlp_layer/pallas_call | solution.py:447
  116.5 2.5 %copy.24 = bf16[128,5120]{1,0:T(8,128)(2,1)} copy(bf16[128,5120]{1,0:T(8,128)(2,1)} %mlp_layer.3) | data formatting | bytes 2621440
